TPU v7x, 8 devices: a whole 2x2x1 slice. The times are simulated.
8 devices in a mesh: dp: 1 (over z), tp2: 2 (over y), tp: 4 (over x, core).
Axes of the slice: x: 2, y: 2, z: 1, core: 2. Of those that a mesh axis runs over, the one named last changes fastest.
Arguments:
- hidden: bfloat16 [1024, 2048], P('dp')
- w_gate: bfloat16 [2048, 8192], P(None, ('tp2', 'tp'))
- w_up: bfloat16 [2048, 8192], P(None, ('tp2', 'tp'))
- w_down: bfloat16 [8192, 2048], P(('tp2', 'tp'))
- norm_gain: float32 [2048], replicated
- w_vocab: bfloat16 [2048, 128256], P(None, ('tp2', 'tp'))
- temperature: float32 [1024], P('dp')
- target_ids: int32 [1024], P('dp')
Outputs:
- output 1: float32 [1024], P('dp')
- output 2: float32 [1024], P('dp')
- output 3: float32 [1024], P('dp')
- output 4: bfloat16 [1024, 128256], P('dp', ('tp2', 'tp'))
All inputs are finite; a program needn't handle non-finite values.
Results may differ from a plain program's by a relative error of at most 0.00345951.
Values are sent between devices in bfloat16 or wider.
A program may use at most 1 GiB of HBM per device.

v0:
```python
import jax
import jax.numpy as jnp
from jax import lax
from jax.sharding import PartitionSpec as P

NORM_EPS = 1e-6


def solution(mesh):
    model_axes = ('tp2', 'tp')
    tp_size = mesh.shape['tp']

    def local_step(hidden, w_gate, w_up, w_down, norm_gain, w_vocab, value_a11, target_ids):
        gate_pre = jnp.dot(hidden, w_gate, preferred_element_type=jnp.float32)
        up_pre = jnp.dot(hidden, w_up, preferred_element_type=jnp.float32)
        hidden_act = (jax.nn.silu(gate_pre) * up_pre).astype(jnp.bfloat16)
        part_out = jnp.dot(hidden_act, w_down, preferred_element_type=jnp.float32).astype(jnp.bfloat16)
        mlp_out = lax.psum(part_out, model_axes)
        resid_sum = hidden.astype(jnp.float32) + mlp_out.astype(jnp.float32)
        inv_rms = lax.rsqrt(jnp.mean(resid_sum * resid_sum, axis=-1, keepdims=True) + NORM_EPS)
        normed = (norm_gain * resid_sum * inv_rms).astype(jnp.bfloat16)
        logits = jnp.dot(normed, w_vocab, preferred_element_type=jnp.float32) / value_a11[:, None]
        shard_cols = logits.shape[1]
        shard_index = lax.axis_index('tp2') * tp_size + lax.axis_index('tp')
        local_max = jnp.max(logits, axis=-1)
        shifted = jnp.exp(logits - local_max[:, None])
        local_sum = jnp.sum(shifted, axis=-1)
        local_moment = jnp.sum(shifted * logits, axis=-1)
        local_ids = target_ids - shard_index * shard_cols
        col_ids = jnp.arange(shard_cols, dtype=jnp.int32)
        local_target = jnp.sum(jnp.where(col_ids[None, :] == local_ids[:, None], logits, 0.0), axis=-1)
        global_max = lax.pmax(local_max, model_axes)
        rescale = jnp.exp(local_max - global_max)
        row_stats = jnp.stack([local_sum * rescale, local_moment * rescale, local_target], axis=0)
        totals = lax.psum(row_stats, model_axes)
        log_norm = global_max + jnp.log(totals[0])
        entropy = log_norm - totals[1] / totals[0]
        target_logp = totals[2] - log_norm
        logprobs = (logits - log_norm[:, None]).astype(jnp.bfloat16)
        return log_norm, entropy, target_logp, logprobs

    return jax.shard_map(
        local_step, mesh=mesh,
        in_specs=(P('dp', None), P(None, model_axes), P(None, model_axes), P(model_axes, None),
                  P(None), P(None, model_axes), P('dp'), P('dp')),
        out_specs=(P('dp'), P('dp'), P('dp'), P('dp', model_axes)),
        check_vma=False)
```

profile of v0, /device:TPU:0, one launch (start us, length us, event | category | flops | bytes accessed | tf_op | source)
XLA Modules:
  0.0 300.9 jit_solution(9402299192475142148)
XLA Ops:
  7.2 0.0 all-reduce.2.cloned.1.call-start
  7.2 10.0 %fusion.8 = f32[1024,1024]{1,0:T(8,128)} fusion(bf16[1024,2048]{1,0:T(8,128)(2,1)} %param.8, bf16[2048,1024]{1,0:T(8,128)(2,1)} %param.9), kind=kOutput, calls=%fused_computation.25 | convolution fusion | flops 4294967296 | bytes 12582912 | tf_op jit(solution)/shard_map/dot_general | solution.py:14
  17.2 15.1 %convolution_convert_fusion = bf16[1024,2048]{1,0:T(8,128)(2,1)} fusion(bf16[1024,2048]{1,0:T(8,128)(2,1)} %param.11, f32[1024,1024]{1,0:T(8,128)} %fusion.8, bf16[1024,2048]{1,0:T(8,128)(2,1)} %param.8, bf16[2048,1024]{1,0:T(8,128)(2,1)} %param.10), kind=kOutput, calls=%fused_computation.13 | convolution fusion | flops 8598323200 | bytes 20971520 | tf_op jit(solution)/shard_map/dot_general | solution.py:17
  32.3 0.0 copy-start.3
  32.3 0.0 all-reduce.2.cloned.1.call-update
  32.3 0.7 copy-done.3
  33.0 0.6 broadcast_subtract_fusion
  33.6 0.0 copy-start.4
  33.6 0.0 copy-start.5
  33.6 71.0 %all-reduce.2.cloned.1.call-done = bf16[1024,2048]{1,0:T(8,128)(2,1)} async-done(((bf16[1024,2048]{1,0:T(8,128)(2,1)}), bf16[1024,2048]{1,0:T(8,128)(2,1)}) %all-reduce.2.cloned.1.call-update) | async-done | bytes 4194320 | tf_op jit(solution)/shard_map/psum | solution.py:18
  104.6 0.0 copy-start
  104.6 5.0 %multiply_reduce_fusion.1 = f32[1024]{0:T(1024)S(1)} fusion(bf16[1024,2048]{1,0:T(8,128)(2,1)} %all-reduce.2.cloned.1.call-done, bf16[1024,2048]{1,0:T(8,128)(2,1)} %param.8), kind=kLoop, calls=%fused_computation.8 | loop fusion | flops 10484736 | bytes 8392704 | tf_op jit(solution)/shard_map/reduce_sum | solution.py:20
  109.6 0.0 copy-done.4
  109.6 0.0 copy-done.5
  109.6 0.0 copy-done
  109.6 0.0 copy-start.2
  109.6 81.2 %fusion.7 = (f32[1024]{0:T(1024)S(1)}, f32[1024,16032]{0,1:T(8,128)}) fusion(f32[1024]{0:T(1024)S(1)} %copy-done.5, bf16[2048,16032]{0,1:T(8,128)(2,1)} %param.13, bf16[1024,2048]{1,0:T(8,128)(2,1)} %all-reduce.2.cloned.1.call-done, bf16[1024,2048]{1,0:T(8,128)(2,1)S(1)} %copy-done, f32[1024]{0:T(1024)S(1)} %add_rsqrt_fusion, f32[2048]{0:T(1024)S(1)} %copy-done.4), kind=kOutput, calls=%fused_computation.24 | convolution fusion | flops 67288498176 | bytes 139743232 | tf_op jit(solution)/shard_map/dot_general | solution.py:22
  190.8 22.3 %pmax.7 = f32[1024]{0:T(1024)S(1)} all-reduce(f32[1024]{0:T(1024)S(1)} %get-tuple-element.14), channel_id=1, replica_groups=mesh['dp'=1,'tp2'=2,'tp'=4] {'tp2','tp'}, use_global_device_ids=true, to_apply=%region_3.4 | all-reduce | flops 1024 | bytes 8192 | tf_op jit(solution)/shard_map/pmax | solution.py:32
  213.1 0.0 copy-done.2
  213.1 23.8 %fusion = (f32[1024]{0:T(1024)S(1)}, f32[1024]{0:T(1024)S(1)}, f32[1024]{0:T(1024)S(1)}) fusion(f32[1024,16032]{0,1:T(8,128)} %get-tuple-element.15, f32[1024]{0:T(1024)S(1)} %get-tuple-element.14, s32[1024]{0:T(1024)S(1)} %copy-done.2), kind=kLoop, calls=%fused_computation.5 | loop fusion | flops 114914304 | bytes 65687552 | tf_op jit(solution)/shard_map/reduce_sum | solution.py:27
  237.0 24.0 %psum.15 = f32[3,1024]{1,0:T(4,128)S(1)} all-reduce(f32[3,1024]{1,0:T(4,128)S(1)} %pad_maximum_fusion), channel_id=1, replica_groups=mesh['dp'=1,'tp2'=2,'tp'=4] {'tp2','tp'}, use_global_device_ids=true, to_apply=%region_7.8 | all-reduce | flops 3072 | bytes 24576 | tf_op jit(solution)/shard_map/psum | solution.py:35
  261.0 0.6 fusion.6
  261.6 0.0 copy-start.1
  261.6 31.9 %subtract_convert_fusion = bf16[1024,16032]{0,1:T(8,128)(2,1)} fusion(f32[1024,16032]{0,1:T(8,128)} %get-tuple-element.15, f32[1024]{0:T(1024)S(1)} %get-tuple-element.8), kind=kLoop, calls=%fused_computation | loop fusion | flops 32833536 | bytes 98504704 | tf_op jit(solution)/shard_map/convert_element_type | solution.py:39
  293.5 0.0 copy-done.1
  293.5 0.6 sub.36
  (4 shorter events, 0.1 us)
Async XLA Ops:
  7.2 97.4 %all-reduce.2.cloned.1.call-start = ((), (), s32[]{:S(2)}) async-start(), calls=%async_computation | async-start | bytes 8388608 | tf_op jit(solution)/shard_map/psum | solution.py:18
  32.3 0.7 copy-start.3
  33.6 76.1 %copy-start.4 = (f32[2048]{0:T(1024)S(1)}, f32[2048]{0:T(1024)}, u32[]{:S(2)}) copy-start(f32[2048]{0:T(1024)} %param.12) | copy-start | bytes 24580
  33.6 76.1 %copy-start.5 = (f32[1024]{0:T(1024)S(1)}, f32[1024]{0:T(1024)}, u32[]{:S(2)}) copy-start(f32[1024]{0:T(1024)} %param.14) | copy-start | bytes 12292
  104.6 5.1 %copy-start = (bf16[1024,2048]{1,0:T(8,128)(2,1)S(1)}, bf16[1024,2048]{1,0:T(8,128)(2,1)}, u32[]{:S(2)}) copy-start(bf16[1024,2048]{1,0:T(8,128)(2,1)} %param.8) | copy-start | bytes 12582916
  109.6 103.5 %copy-start.2 = (s32[1024]{0:T(1024)S(1)}, s32[1024]{0:T(1024)}, u32[]{:S(2)}) copy-start(s32[1024]{0:T(1024)} %broadcast_subtract_fusion) | copy-start | bytes 12292
  261.6 31.9 %copy-start.1 = (f32[1024]{0:T(1024)}, f32[1024]{0:T(1024)S(1)}, u32[]{:S(2)}) copy-start(f32[1024]{0:T(1024)S(1)} %get-tuple-element.8) | copy-start | bytes 12292
Sparse Core Ops, SparseCore 0:
  32.4 72.1 all-reduce.1
where the time goes:
time: 301 us
  matrix products  106 us (35%)
  waiting for transfers between devices  71 us (24%)
  other arithmetic  62.5 us (21%)
  blocking collectives  46.3 us (15%)
  between operations  14.1 us (5%)
    dot_general x1, matrix products, local_step(): jnp.dot(normed, w_vocab, preferred_element_type=jnp.float32)  81.2 us
    psum x1, waiting for transfers between devices, local_step(): mlp_out = lax.psum(part_out, model_axes)  71 us
    convert_element_type x1, other arithmetic, local_step(): logprobs = (logits - log_norm[:, None]).astype(jnp.bfloat16)  31.9 us
    psum x1, blocking collectives, local_step(): totals = lax.psum(row_stats, model_axes)  24 us
    reduce_sum x1, other arithmetic, local_step(): local_sum = jnp.sum(shifted, axis=-1)  23.8 us
    pmax x1, blocking collectives, local_step(): global_max = lax.pmax(local_max, model_axes)  22.3 us
    dot_general x1, matrix products, local_step(): jnp.dot(hidden_act, w_down, preferred_element_type=jnp.float32)  15.1 us
    dot_general x1, matrix products, local_step(): gate_pre = jnp.dot(hidden, w_gate, preferred_element_type=jnp.float32)  9.97 us
  transfers between devices with their start and end apart: 1, of which 1 were waited for; matrix products, arithmetic and copies ran while one was open for 0% of the time, Pallas kernels for 0%

commit v1 on v0

v1 whole, which is shorter than its diff:
```python
import functools

import jax
import jax.numpy as jnp
from jax import lax
from jax.experimental import pallas as pl
from jax.experimental.pallas import tpu as pltpu
from jax.sharding import PartitionSpec as P

NORM_EPS = 1e-6
VM = pltpu.VMEM
MESH = pl.DeviceIdType.MESH
V = 16032
R = 512
BV = 1024
NT = V // BV
REM = V - NT * BV
SB = 512
NB = 3
MIB = 2 ** 20


def head_tile(w_ref, x_ref, l_ref, st_ref, row0, bv, inv_t, ids, fin=None):
    off = 0
    while off < bv:
        sb = min(SB, bv - off)
        rows = pl.ds(row0 + off, sb)
        if fin is not None:
            stage, log_norm = fin
            stage[pl.ds(off, sb), :] = (l_ref[rows, :] - log_norm).astype(jnp.bfloat16)
        logits = lax.dot_general(w_ref[pl.ds(off, sb), :], x_ref[...], (((1,), (1,)), ((), ())),
                                 preferred_element_type=jnp.float32) * inv_t
        l_ref[rows, :] = logits
        l3 = logits.reshape(sb // 8, 8, R)
        m_old = st_ref[0]
        m_new = jnp.maximum(m_old, jnp.max(l3, axis=0))
        scale = jnp.exp(m_old - m_new)
        e = jnp.exp(l3 - m_new[None])
        pos = lax.broadcasted_iota(jnp.int32, (sb // 8, 8, R), 0) * 8 + lax.broadcasted_iota(jnp.int32, (sb // 8, 8, R), 1)
        hit = pos == (ids - (row0 + off))[None]
        st_ref[0] = m_new
        st_ref[1] = st_ref[1] * scale + jnp.sum(e, axis=0)
        st_ref[2] = st_ref[2] * scale + jnp.sum(e * l3, axis=0)
        st_ref[3] = st_ref[3] + jnp.sum(jnp.where(hit, l3, 0.0), axis=0)
        off += sb


def init_stats(st_ref):
    st_ref[0] = jnp.full((8, R), -3.0e38, jnp.float32)
    st_ref[1] = jnp.zeros((8, R), jnp.float32)
    st_ref[2] = jnp.zeros((8, R), jnp.float32)
    st_ref[3] = jnp.zeros((8, R), jnp.float32)


def reduce_stats(st_ref, out_ref):
    m = jnp.max(st_ref[0], axis=0, keepdims=True)
    scale = jnp.exp(st_ref[0] - m)
    out_ref[0:1, :] = m
    out_ref[1:2, :] = jnp.sum(st_ref[1] * scale, axis=0, keepdims=True)
    out_ref[2:3, :] = jnp.sum(st_ref[2] * scale, axis=0, keepdims=True)
    out_ref[3:4, :] = jnp.sum(st_ref[3], axis=0, keepdims=True)
    out_ref[4:8, :] = jnp.zeros((4, R), jnp.float32)


def w_copy(wt_ref, wbuf, sems, tile, size):
    slot = lax.rem(tile, NB) if not isinstance(tile, int) else tile % NB
    return pltpu.make_async_copy(wt_ref.at[pl.ds(tile * BV, size)], wbuf.at[slot, pl.ds(0, size)], sems.at[slot])


def w_start(wt_ref, wbuf, sems, tile):
    @pl.when(tile < NT)
    def _():
        w_copy(wt_ref, wbuf, sems, tile, BV).start()

    @pl.when(tile == NT)
    def _():
        w_copy(wt_ref, wbuf, sems, tile, REM).start()


def head_kernel(half, last_half, *refs):
    if last_half:
        (x_ref, wt_ref, t_ref, ids_ref, res_ref, l_in, o_ref, l_ref, stat_ref,
         wbuf, st_ref, wsem, stage, osem) = refs
    else:
        x_ref, wt_ref, t_ref, ids_ref, l_ref, stat_ref, wbuf, st_ref, wsem = refs
    for t in range(NB - 1):
        w_copy(wt_ref, wbuf, wsem, t, BV).start()
    init_stats(st_ref)
    me = lax.axis_index('tp2') * 4 + lax.axis_index('tp')
    inv_t = 1.0 / t_ref[:, half * R:(half + 1) * R]
    ids = ids_ref[:, half * R:(half + 1) * R] - me * V
    x = x_ref.at[pl.ds(half * R, R)]

    def out_copy(tile, size):
        slot = lax.rem(tile, 2) if not isinstance(tile, int) else tile % 2
        return pltpu.make_async_copy(stage.at[slot, pl.ds(0, size)],
                                     o_ref.at[pl.ds(tile * BV, size), pl.ds((1 - half) * R, R)], osem.at[slot])

    def step(tile, size):
        slot = lax.rem(tile, NB) if not isinstance(tile, int) else tile % NB
        w_copy(wt_ref, wbuf, wsem, tile, size).wait()
        if not isinstance(tile, int):
            w_start(wt_ref, wbuf, wsem, tile + NB - 1)
        fin = None
        if last_half:
            oslot = lax.rem(tile, 2) if not isinstance(tile, int) else tile % 2
            if isinstance(tile, int):
                out_copy(tile - 2, BV).wait()
            else:
                @pl.when(tile >= 2)
                def _():
                    out_copy(tile - 2, BV).wait()
            fin = (stage.at[oslot], res_ref[0:1, :])
        row0 = tile * BV if isinstance(tile, int) else pl.multiple_of(tile * BV, BV)
        head_tile(wbuf.at[slot], x, l_ref, st_ref, row0, size, inv_t, ids, fin)
        if last_half:
            out_copy(tile, size).start()

    def body(i, _):
        step(i, BV)
        return 0

    lax.fori_loop(0, NT, body, 0)
    step(NT, REM)
    reduce_stats(st_ref, stat_ref)
    if last_half:
        out_copy(NT - 1, BV).wait()
        out_copy(NT, REM).wait()


def exchange_kernel(s_ref, res_ref, box, send_sem, recv_sem):
    a, b = lax.axis_index('tp2'), lax.axis_index('tp')
    bar = pltpu.get_barrier_semaphore()
    peers = [(i, j) for i in range(2) for j in range(4) if (i, j) != (0, 0)]

    def peer(d):
        return {'tp2': lax.rem(a + d[0], 2), 'tp': lax.rem(b + d[1], 4)}

    for d in peers:
        pl.semaphore_signal(bar, inc=1, device_id=peer(d), device_id_type=MESH)
    pl.semaphore_wait(bar, 7)
    copies = []
    for n, d in enumerate(peers):
        c = pltpu.make_async_remote_copy(s_ref, box.at[n], send_sem.at[n], recv_sem.at[n],
                                         device_id=peer(d), device_id_type=MESH)
        c.start()
        copies.append(c)
    for c in copies:
        c.wait()
    m = s_ref[0:1, :]
    for n in range(7):
        m = jnp.maximum(m, box[n, 0:1, :])
    k = jnp.exp(s_ref[0:1, :] - m)
    s, q, t = s_ref[1:2, :] * k, s_ref[2:3, :] * k, s_ref[3:4, :]
    for n in range(7):
        k = jnp.exp(box[n, 0:1, :] - m)
        s += box[n, 1:2, :] * k
        q += box[n, 2:3, :] * k
        t += box[n, 3:4, :]
    log_norm = m + jnp.log(s)
    res_ref[0:1, :] = log_norm
    res_ref[1:2, :] = log_norm - q / s
    res_ref[2:3, :] = t - log_norm
    res_ref[3:8, :] = jnp.zeros((5, R), jnp.float32)


def finish_kernel(l_ref, r0_ref, r1_ref, o_in, o_ref, ln_ref, en_ref, tl_ref, stage, osem):
    for half, r in ((0, r0_ref), (1, r1_ref)):
        cols = slice(half * R, (half + 1) * R)
        ln_ref[:, cols] = r[0:1, :]
        en_ref[:, cols] = r[1:2, :]
        tl_ref[:, cols] = r[2:3, :]
    log_norm = r1_ref[0:1, :]

    def out_copy(tile, size):
        slot = lax.rem(tile, 4) if not isinstance(tile, int) else tile % 4
        return pltpu.make_async_copy(stage.at[slot, pl.ds(0, size)],
                                     o_ref.at[pl.ds(tile * BV, size), pl.ds(R, R)], osem.at[slot])

    def step(tile, size):
        slot = lax.rem(tile, 4) if not isinstance(tile, int) else tile % 4
        if isinstance(tile, int):
            out_copy(tile - 4, BV).wait()
        else:
            @pl.when(tile >= 4)
            def _():
                out_copy(tile - 4, BV).wait()
        row0 = tile * BV if isinstance(tile, int) else pl.multiple_of(tile * BV, BV)
        stage[slot, 0:size, :] = (l_ref[pl.ds(row0, size), :] - log_norm).astype(jnp.bfloat16)
        out_copy(tile, size).start()

    def body(i, _):
        step(i, BV)
        return 0

    lax.fori_loop(0, NT, body, 0)
    step(NT, REM)
    for t in range(NT - 3, NT):
        out_copy(t, BV).wait()
    out_copy(NT, REM).wait()


def vspec():
    return pl.BlockSpec(memory_space=VM)


def aspec():
    return pl.BlockSpec(memory_space=pl.ANY)


def in_vmem(x):
    return pltpu.with_memory_space_constraint(x, VM)


def params(limit, **kw):
    return pltpu.CompilerParams(has_side_effects=True, vmem_limit_bytes=limit, **kw)


def head_call(half, x, wt, temp, ids, res=None, logits=None):
    last = res is not None
    l_type = VM((V, R), jnp.float32)
    stat_type = jax.ShapeDtypeStruct((8, R), jnp.float32)
    scratch = [VM((NB, BV, 2048), jnp.bfloat16), VM((4, 8, R), jnp.float32), pltpu.SemaphoreType.DMA((NB,))]
    if last:
        args = (x, wt, temp, ids, res, in_vmem(logits))
        in_specs = [vspec(), aspec(), vspec(), vspec(), vspec(), vspec()]
        out_shape = (jax.ShapeDtypeStruct((V, 2 * R), jnp.bfloat16), l_type, stat_type)
        out_specs = (aspec(), vspec(), vspec())
        scratch += [VM((2, BV, R), jnp.bfloat16), pltpu.SemaphoreType.DMA((2,))]
        alias = {5: 1}
    else:
        args = (x, wt, temp, ids)
        in_specs = [vspec(), aspec(), vspec(), vspec()]
        out_shape = (l_type, stat_type)
        out_specs = (vspec(), vspec())
        alias = {}
    return pl.pallas_call(
        functools.partial(head_kernel, half, last), out_shape=out_shape, in_specs=in_specs, out_specs=out_specs,
        scratch_shapes=scratch, input_output_aliases=alias, name='head%d' % half, compiler_params=params(24 * MIB),
        cost_estimate=pl.CostEstimate(flops=2 * V * R * 2048, bytes_accessed=V * 4096, transcendentals=V * R))(*args)


def exchange_call(stats, cid):
    return pl.pallas_call(
        exchange_kernel, out_shape=jax.ShapeDtypeStruct((8, R), jnp.float32), in_specs=[vspec()], out_specs=vspec(),
        scratch_shapes=[VM((7, 8, R), jnp.float32), pltpu.SemaphoreType.DMA((7,)), pltpu.SemaphoreType.DMA((7,))],
        name='exchange%d' % cid, compiler_params=params(8 * MIB, collective_id=cid))(stats)


def finish_call(logits, r0, r1, out):
    row = jax.ShapeDtypeStruct((1, 2 * R), jnp.float32)
    return pl.pallas_call(
        finish_kernel, out_shape=(jax.ShapeDtypeStruct((V, 2 * R), jnp.bfloat16), row, row, row),
        in_specs=[vspec(), vspec(), vspec(), aspec()], out_specs=(aspec(), vspec(), vspec(), vspec()),
        scratch_shapes=[VM((4, BV, R), jnp.bfloat16), pltpu.SemaphoreType.DMA((4,))],
        input_output_aliases={3: 0}, name='finish', compiler_params=params(12 * MIB))(in_vmem(logits), r0, r1, out)


def solution(mesh):
    model_axes = ('tp2', 'tp')

    def local_step(hidden, w_gate, w_up, w_down, norm_gain, w_vocab, temperature, target_ids):
        gate_pre = jnp.dot(hidden, w_gate, preferred_element_type=jnp.float32)
        up_pre = jnp.dot(hidden, w_up, preferred_element_type=jnp.float32)
        hidden_act = (jax.nn.silu(gate_pre) * up_pre).astype(jnp.bfloat16)
        part_out = jnp.dot(hidden_act, w_down, preferred_element_type=jnp.float32).astype(jnp.bfloat16)
        mlp_out = lax.psum(part_out, model_axes)
        resid_sum = hidden.astype(jnp.float32) + mlp_out.astype(jnp.float32)
        inv_rms = lax.rsqrt(jnp.mean(resid_sum * resid_sum, axis=-1, keepdims=True) + NORM_EPS)
        x = (norm_gain * resid_sum * inv_rms).astype(jnp.bfloat16)
        temp = temperature.reshape(1, 2 * R)
        ids = target_ids.reshape(1, 2 * R)
        wt = w_vocab.T
        l0, s0 = head_call(0, x, wt, temp, ids)
        r0 = exchange_call(s0, 1)
        out, l1, s1 = head_call(1, x, wt, temp, ids, r0, l0)
        r1 = exchange_call(s1, 2)
        out, ln, en, tl = finish_call(l1, r0, r1, out)
        return ln.reshape(-1), en.reshape(-1), tl.reshape(-1), out.T

    return jax.shard_map(
        local_step, mesh=mesh,
        in_specs=(P('dp', None), P(None, model_axes), P(None, model_axes), P(model_axes, None),
                  P(None), P(None, model_axes), P('dp'), P('dp')),
        out_specs=(P('dp'), P('dp'), P('dp'), P('dp', model_axes)),
        check_vma=False)
```

time: 301 us -> 271 us (0.900)
  Pallas kernels: 0 us -> 126 us
  matrix products: 106 us -> 25.1 us
  other arithmetic: 62.5 us -> 8.95 us
  blocking collectives: 46.3 us -> 0 us
  local copies, waits for them, and re-layouts: 0.68 us -> 24.1 us
    pallas_call x0 -> x5, Pallas kernels: none -> 126 us  [the longest x2 109 us: head_call(): pl.pallas_call(functools.partial(head_kernel, half, last), out_shape=out_...]
    dot_general x1 -> x0, matrix products: 81.2 us -> none  [local_step(): jnp.dot(normed, w_vocab, preferred_element_type=jnp.float32)]
    convert_element_type x1, other arithmetic: 31.9 us -> 3.92 us  [local_step(): x = (norm_gain * resid_sum * inv_rms).astype(jnp.bfloat16)]
    psum x1 -> x0, blocking collectives: 24 us -> none  [local_step(): totals = lax.psum(row_stats, model_axes)]
    reduce_sum x1 -> x0, other arithmetic: 23.8 us -> none  [local_step(): local_sum = jnp.sum(shifted, axis=-1)]
    unnamed x12 -> x18, local copies, waits for them, and re-layouts: 0.68 us -> 24.1 us
    pmax x1 -> x0, blocking collectives: 22.3 us -> none  [local_step(): global_max = lax.pmax(local_max, model_axes)]
where the time goes in v1:
time: 271 us
  Pallas kernels  126 us (46%)
  waiting for transfers between devices  72.3 us (27%)
  matrix products  25.1 us (9%)
  local copies, waits for them, and re-layouts  24.1 us (9%)
  between operations  14.2 us (5%)
  other arithmetic  8.95 us (3%)
    pallas_call x2, Pallas kernels, head_call(): pl.pallas_call(functools.partial(head_kernel, half, last), out_shape=out_...  109 us
    psum x1, waiting for transfers between devices, local_step(): mlp_out = lax.psum(part_out, model_axes)  72.3 us
    unnamed x18, local copies, waits for them, and re-layouts  24.1 us
    dot_general x1, matrix products, local_step(): jnp.dot(hidden_act, w_down, preferred_element_type=jnp.float32)  15.2 us
    pallas_call x2, Pallas kernels, exchange_call(): pl.pallas_call(exchange_kernel, out_shape=jax.ShapeDtypeStruct((8, R), jn...  10.6 us
    dot_general x1, matrix products, local_step(): gate_pre = jnp.dot(hidden, w_gate, preferred_element_type=jnp.float32)  9.97 us
    pallas_call x1, Pallas kernels, finish_call(): pl.pallas_call(finish_kernel, out_shape=(jax.ShapeDtypeStruct((V, 2 * R),...  6.44 us
  transfers between devices with their start and end apart: 1, of which 1 were waited for; matrix products, arithmetic and copies ran while one was open for 0% of the time, Pallas kernels for 0%

profile of v1, /device:TPU:0, one launch (start us, length us, event | category | flops | bytes accessed | tf_op | source)
XLA Modules:
  0.0 270.7 jit_solution(12702879471853434324)
XLA Ops:
  7.2 0.0 all-reduce.2.cloned.1.call-start
  7.2 10.0 %fusion.1 = f32[1024,1024]{1,0:T(8,128)} fusion(bf16[1024,2048]{1,0:T(8,128)(2,1)} %param.8, bf16[2048,1024]{1,0:T(8,128)(2,1)} %param.9), kind=kOutput, calls=%fused_computation.7 | convolution fusion | flops 4294967296 | bytes 12582912 | tf_op jit(solution)/shard_map/dot_general | solution.py:263
  17.2 15.2 %convolution_convert_fusion = bf16[1024,2048]{1,0:T(8,128)(2,1)} fusion(bf16[1024,2048]{1,0:T(8,128)(2,1)} %param.11, f32[1024,1024]{1,0:T(8,128)} %fusion.1, bf16[1024,2048]{1,0:T(8,128)(2,1)} %param.8, bf16[2048,1024]{1,0:T(8,128)(2,1)} %param.10), kind=kOutput, calls=%fused_computation.4 | convolution fusion | flops 8598323200 | bytes 20971520 | tf_op jit(solution)/shard_map/dot_general | solution.py:266
  32.3 0.0 all-reduce.2.cloned.1.call-update
  32.4 0.0 copy-start.8
  32.4 72.3 %all-reduce.2.cloned.1.call-done = bf16[1024,2048]{1,0:T(8,128)(2,1)} async-done(((bf16[1024,2048]{1,0:T(8,128)(2,1)}), bf16[1024,2048]{1,0:T(8,128)(2,1)}) %all-reduce.2.cloned.1.call-update) | async-done | bytes 4194320 | tf_op jit(solution)/shard_map/psum | solution.py:267
  104.6 0.0 copy-start.6
  104.6 0.0 copy-start.7
  104.6 5.0 %multiply_reduce_fusion = f32[1024]{0:T(1024)S(1)} fusion(bf16[1024,2048]{1,0:T(8,128)(2,1)} %all-reduce.2.cloned.1.call-done, bf16[1024,2048]{1,0:T(8,128)(2,1)} %param.8), kind=kLoop, calls=%fused_computation.1 | loop fusion | flops 10484736 | bytes 8392704 | tf_op jit(solution)/shard_map/reduce_sum | solution.py:269
  109.7 0.0 copy-done.8
  109.7 0.0 copy-done.6
  109.7 0.9 copy-done.7
  110.6 3.9 %multiply_convert_fusion.refs_0_ = bf16[1024,2048]{1,0:T(8,128)(2,1)} fusion(bf16[1024,2048]{1,0:T(8,128)(2,1)S(1)} %copy-done.7, bf16[1024,2048]{1,0:T(8,128)(2,1)S(1)} %copy-done.6, f32[1024]{0:T(1024)S(1)} %add_rsqrt_fusion, f32[2048]{0:T(1024)S(1)} %copy-done.8), kind=kLoop, calls=%fused_computation | loop fusion | flops 12582912 | bytes 12595200 | tf_op jit(solution)/shard_map/convert_element_type | solution.py:270
  114.5 52.4 %head0.1 = (f32[16032,512]{1,0:T(8,128)S(1)}, f32[8,512]{1,0:T(8,128)}) custom-call(bf16[1024,2048]{1,0:T(8,128)(2,1)} %multiply_convert_fusion.refs_0_, bf16[16032,2048]{1,0:T(8,128)(2,1)} %bitcast.13, f32[1,1024]{1,0:T(1,128)} %bitcast.15, s32[1,1024]{1,0:T(1,128)} %bitcast.17), custom_call_target="tpu_custom_call" | custom-call | flops 33621540864 | bytes 65667072 | tf_op jit(solution)/shard_map/head0/pallas_call | solution.py:237
  166.9 0.0 copy-start.5
  166.9 0.7 copy-done.5
  167.6 5.3 %exchange1.1.refs_4_.r0_ref = f32[8,512]{1,0:T(8,128)S(1)} custom-call(f32[8,512]{1,0:T(8,128)S(1)} %copy-done.5), custom_call_target="tpu_custom_call" | custom-call | tf_op jit(solution)/shard_map/exchange1/pallas_call | solution.py:244
  172.9 0.0 copy-start.2
  172.9 0.6 copy-done.2
  173.5 0.0 copy-start.3
  173.5 56.6 %head1.1 = (bf16[16032,1024]{1,0:T(8,128)(2,1)}, f32[16032,512]{1,0:T(8,128)S(1)}, f32[8,512]{1,0:T(8,128)}) custom-call(bf16[1024,2048]{1,0:T(8,128)(2,1)} %multiply_convert_fusion.refs_0_, bf16[16032,2048]{1,0:T(8,128)(2,1)} %bitcast.14, f32[1,1024]{1,0:T(1,128)} %bitcast.16, s32[1,1024]{1,0:T(1,128)} %bitcast.18, ...), custom_call_target="tpu_custom_call", output_to_operand_aliasing={{1}: (5, {})} | custom-call | flops 33621540864 | bytes 65667072 | tf_op jit(solution)/shard_map/head1/pallas_call | solution.py:237
  230.2 0.0 copy-start
  230.2 10.8 %copy-done = f32[16032,512]{1,0:T(8,128)} copy-done((f32[16032,512]{1,0:T(8,128)}, f32[16032,512]{1,0:T(8,128)S(1)}, u32[]{:S(2)}) %copy-start) | copy-done | bytes 32833560
  241.0 0.0 copy-start.4
  241.0 0.7 copy-done.4
  241.7 5.3 %exchange2.1.r1_ref = f32[8,512]{1,0:T(8,128)S(1)} custom-call(f32[8,512]{1,0:T(8,128)S(1)} %copy-done.4), custom_call_target="tpu_custom_call" | custom-call | tf_op jit(solution)/shard_map/exchange2/pallas_call | solution.py:244
  247.0 0.0 copy-done.3
  247.0 0.0 copy-start.1
  247.1 10.3 %copy-done.1 = f32[16032,512]{1,0:T(8,128)S(1)} copy-done((f32[16032,512]{1,0:T(8,128)S(1)}, f32[16032,512]{1,0:T(8,128)}, u32[]{:S(2)}) %copy-start.1) | copy-done | bytes 32833560
  257.4 6.4 %finish.1 = (bf16[16032,1024]{1,0:T(8,128)(2,1)}, f32[1,1024]{1,0:T(1,128)}, f32[1,1024]{1,0:T(1,128)}, f32[1,1024]{1,0:T(1,128)}) custom-call(f32[16032,512]{1,0:T(8,128)S(1)} %copy-done.1, f32[8,512]{1,0:T(8,128)S(1)} %copy-done.3, f32[8,512]{1,0:T(8,128)S(1)} %exchange2.1.r1_ref, ...), custom_call_target="tpu_custom_call", output_to_operand_aliasing={{0}: (3, {})} | custom-call | tf_op jit(solution)/shard_map/finish/pallas_call | solution.py:252
  (1 shorter events, 0.0 us)
Async XLA Ops:
  7.2 97.5 %all-reduce.2.cloned.1.call-start = ((), (), s32[]{:S(2)}) async-start(), calls=%async_computation | async-start | bytes 8388608 | tf_op jit(solution)/shard_map/psum | solution.py:267
  32.4 77.3 %copy-start.8 = (f32[2048]{0:T(1024)S(1)}, f32[2048]{0:T(1024)}, u32[]{:S(2)}) copy-start(f32[2048]{0:T(1024)} %param.12) | copy-start | bytes 24580
  104.6 5.1 %copy-start.6 = (bf16[1024,2048]{1,0:T(8,128)(2,1)S(1)}, bf16[1024,2048]{1,0:T(8,128)(2,1)}, u32[]{:S(2)}) copy-start(bf16[1024,2048]{1,0:T(8,128)(2,1)} %param.8) | copy-start | bytes 12582916
  104.6 5.9 %copy-start.7 = (bf16[1024,2048]{1,0:T(8,128)(2,1)S(1)}, bf16[1024,2048]{1,0:T(8,128)(2,1)}, u32[]{:S(2)}) copy-start(bf16[1024,2048]{1,0:T(8,128)(2,1)} %all-reduce.2.cloned.1.call-done) | copy-start | bytes 12582916
  166.9 0.7 copy-start.5
  172.9 0.6 copy-start.2
  173.5 73.5 %copy-start.3 = (f32[8,512]{1,0:T(8,128)S(1)}, f32[8,512]{1,0:T(8,128)}, u32[]{:S(2)}) copy-start(f32[8,512]{1,0:T(8,128)} %copy-done.2) | copy-start | bytes 49156
  230.2 10.8 %copy-start = (f32[16032,512]{1,0:T(8,128)}, f32[16032,512]{1,0:T(8,128)S(1)}, u32[]{:S(2)}) copy-start(f32[16032,512]{1,0:T(8,128)S(1)} %get-tuple-element.15.l_ref) | copy-start | bytes 98500608
  241.0 0.7 copy-start.4
  247.0 10.3 %copy-start.1 = (f32[16032,512]{1,0:T(8,128)S(1)}, f32[16032,512]{1,0:T(8,128)}, u32[]{:S(2)}) copy-start(f32[16032,512]{1,0:T(8,128)} %copy-done) | copy-start | bytes 98500608
Sparse Core Ops, SparseCore 0:
  32.5 72.1 all-reduce.1

commit v2 on v1

--- a/solution.py
+++ b/solution.py
@@ -15,34 +15,51 @@
 BV = 1024
 NT = V // BV
 REM = V - NT * BV
-SB = 512
+SB = 256
+SLICE = 128
 NB = 3
 MIB = 2 ** 20
-
-
-def head_tile(w_ref, x_ref, l_ref, st_ref, row0, bv, inv_t, ids, fin=None):
-    off = 0
+LIMIT = 26 * MIB
+
+
+def block_stats(l_ref, st_ref, row0, sb, ids, valid=None):
+    for c in range(0, R, 128):
+        lanes = slice(c, c + 128)
+        m_old, s_old, q_old, t_old = (st_ref[n, :, lanes] for n in range(4))
+        m, s, q, t = m_old, s_old, q_old, t_old
+        for r in range(0, sb, SLICE):
+            n = min(SLICE, sb - r) // 8
+            l3 = l_ref[pl.ds(row0 + r, n * 8), lanes].reshape(n, 8, 128)
+            m_new = jnp.maximum(m, jnp.max(l3, axis=0))
+            scale = jnp.exp(m - m_new)
+            e = jnp.exp(l3 - m_new[None])
+            shape = (n, 8, 128)
+            pos = lax.broadcasted_iota(jnp.int32, shape, 0) * 8 + lax.broadcasted_iota(jnp.int32, shape, 1)
+            hit = pos == (ids[:, lanes] - (row0 + r - SB))[None]
+            s = s * scale + jnp.sum(e, axis=0)
+            q = q * scale + jnp.sum(e * l3, axis=0)
+            t = t + jnp.sum(jnp.where(hit, l3, 0.0), axis=0)
+            m = m_new
+        if valid is not None:
+            m, s = jnp.where(valid, m, m_old), jnp.where(valid, s, s_old)
+            q, t = jnp.where(valid, q, q_old), jnp.where(valid, t, t_old)
+        st_ref[0, :, lanes], st_ref[1, :, lanes], st_ref[2, :, lanes], st_ref[3, :, lanes] = m, s, q, t
+
+
+def head_tile(w_ref, x_ref, l_ref, st_ref, row0, bv, inv_t, ids, fin=None, valid=None):
+    off, prev = 0, SB
     while off < bv:
         sb = min(SB, bv - off)
-        rows = pl.ds(row0 + off, sb)
+        rows = pl.ds(row0 + SB + off, sb)
         if fin is not None:
             stage, log_norm = fin
             stage[pl.ds(off, sb), :] = (l_ref[rows, :] - log_norm).astype(jnp.bfloat16)
         logits = lax.dot_general(w_ref[pl.ds(off, sb), :], x_ref[...], (((1,), (1,)), ((), ())),
                                  preferred_element_type=jnp.float32) * inv_t
+        block_stats(l_ref, st_ref, row0 + SB + off - prev, prev, ids, valid if off == 0 else None)
         l_ref[rows, :] = logits
-        l3 = logits.reshape(sb // 8, 8, R)
-        m_old = st_ref[0]
-        m_new = jnp.maximum(m_old, jnp.max(l3, axis=0))
-        scale = jnp.exp(m_old - m_new)
-        e = jnp.exp(l3 - m_new[None])
-        pos = lax.broadcasted_iota(jnp.int32, (sb // 8, 8, R), 0) * 8 + lax.broadcasted_iota(jnp.int32, (sb // 8, 8, R), 1)
-        hit = pos == (ids - (row0 + off))[None]
-        st_ref[0] = m_new
-        st_ref[1] = st_ref[1] * scale + jnp.sum(e, axis=0)
-        st_ref[2] = st_ref[2] * scale + jnp.sum(e * l3, axis=0)
-        st_ref[3] = st_ref[3] + jnp.sum(jnp.where(hit, l3, 0.0), axis=0)
-        off += sb
+        off, prev = off + sb, sb
+    return prev
 
 
 def init_stats(st_ref):
@@ -112,7 +129,10 @@
                     out_copy(tile - 2, BV).wait()
             fin = (stage.at[oslot], res_ref[0:1, :])
         row0 = tile * BV if isinstance(tile, int) else pl.multiple_of(tile * BV, BV)
-        head_tile(wbuf.at[slot], x, l_ref, st_ref, row0, size, inv_t, ids, fin)
+        valid = None if isinstance(tile, int) else tile > 0
+        prev = head_tile(wbuf.at[slot], x, l_ref, st_ref, row0, size, inv_t, ids, fin, valid)
+        if isinstance(tile, int):
+            block_stats(l_ref, st_ref, row0 + SB + size - prev, prev, ids)
         if last_half:
             out_copy(tile, size).start()
 
@@ -186,7 +206,7 @@
             def _():
                 out_copy(tile - 4, BV).wait()
         row0 = tile * BV if isinstance(tile, int) else pl.multiple_of(tile * BV, BV)
-        stage[slot, 0:size, :] = (l_ref[pl.ds(row0, size), :] - log_norm).astype(jnp.bfloat16)
+        stage[slot, 0:size, :] = (l_ref[pl.ds(row0 + SB, size), :] - log_norm).astype(jnp.bfloat16)
         out_copy(tile, size).start()
 
     def body(i, _):
@@ -218,7 +238,7 @@
 
 def head_call(half, x, wt, temp, ids, res=None, logits=None):
     last = res is not None
-    l_type = VM((V, R), jnp.float32)
+    l_type = VM((V + SB, R), jnp.float32)
     stat_type = jax.ShapeDtypeStruct((8, R), jnp.float32)
     scratch = [VM((NB, BV, 2048), jnp.bfloat16), VM((4, 8, R), jnp.float32), pltpu.SemaphoreType.DMA((NB,))]
     if last:
@@ -236,7 +256,7 @@
         alias = {}
     return pl.pallas_call(
         functools.partial(head_kernel, half, last), out_shape=out_shape, in_specs=in_specs, out_specs=out_specs,
-        scratch_shapes=scratch, input_output_aliases=alias, name='head%d' % half, compiler_params=params(24 * MIB),
+        scratch_shapes=scratch, input_output_aliases=alias, name='head%d' % half, compiler_params=params(LIMIT),
         cost_estimate=pl.CostEstimate(flops=2 * V * R * 2048, bytes_accessed=V * 4096, transcendentals=V * R))(*args)
 
 
@@ -244,7 +264,7 @@
     return pl.pallas_call(
         exchange_kernel, out_shape=jax.ShapeDtypeStruct((8, R), jnp.float32), in_specs=[vspec()], out_specs=vspec(),
         scratch_shapes=[VM((7, 8, R), jnp.float32), pltpu.SemaphoreType.DMA((7,)), pltpu.SemaphoreType.DMA((7,))],
-        name='exchange%d' % cid, compiler_params=params(8 * MIB, collective_id=cid))(stats)
+        name='exchange%d' % cid, compiler_params=params(LIMIT, collective_id=cid))(stats)
 
 
 def finish_call(logits, r0, r1, out):
@@ -253,7 +273,7 @@
         finish_kernel, out_shape=(jax.ShapeDtypeStruct((V, 2 * R), jnp.bfloat16), row, row, row),
         in_specs=[vspec(), vspec(), vspec(), aspec()], out_specs=(aspec(), vspec(), vspec(), vspec()),
         scratch_shapes=[VM((4, BV, R), jnp.bfloat16), pltpu.SemaphoreType.DMA((4,))],
-        input_output_aliases={3: 0}, name='finish', compiler_params=params(12 * MIB))(in_vmem(logits), r0, r1, out)
+        input_output_aliases={3: 0}, name='finish', compiler_params=params(LIMIT))(in_vmem(logits), r0, r1, out)
 
 
 def solution(mesh):

time: 271 us -> 248 us (0.915)
  local copies, waits for them, and re-layouts: 24.1 us -> 3.48 us
    unnamed x18 -> x14, local copies, waits for them, and re-layouts: 24.1 us -> 3.48 us
    pallas_call x2, Pallas kernels: 109 us -> 106 us  [head_call(): pl.pallas_call(functools.partial(head_kernel, half, last), out_shape=out_...]
where the time goes in v2:
time: 248 us
  Pallas kernels  124 us (50%)
  waiting for transfers between devices  72.3 us (29%)
  matrix products  25.1 us (10%)
  between operations  14.1 us (6%)
  other arithmetic  8.96 us (4%)
  local copies, waits for them, and re-layouts  3.48 us (1%)
    pallas_call x2, Pallas kernels, head_call(): pl.pallas_call(functools.partial(head_kernel, half, last), out_shape=out_...  106 us
    psum x1, waiting for transfers between devices, local_step(): mlp_out = lax.psum(part_out, model_axes)  72.3 us
    dot_general x1, matrix products, local_step(): jnp.dot(hidden_act, w_down, preferred_element_type=jnp.float32)  15.2 us
    pallas_call x2, Pallas kernels, exchange_call(): pl.pallas_call(exchange_kernel, out_shape=jax.ShapeDtypeStruct((8, R), jn...  10.6 us
    dot_general x1, matrix products, local_step(): gate_pre = jnp.dot(hidden, w_gate, preferred_element_type=jnp.float32)  9.97 us
    pallas_call x1, Pallas kernels, finish_call(): pl.pallas_call(finish_kernel, out_shape=(jax.ShapeDtypeStruct((V, 2 * R),...  7.18 us
    reduce_sum x1, other arithmetic, local_step(): jnp.mean(resid_sum * resid_sum, axis=-1, keepdims=True) + NORM_EPS  5.02 us
  transfers between devices with their start and end apart: 1, of which 1 were waited for; matrix products, arithmetic and copies ran while one was open for 0% of the time, Pallas kernels for 0%

profile of v2, /device:TPU:0, one launch (start us, length us, event | category | flops | bytes accessed | tf_op | source)
XLA Modules:
  0.0 248.1 jit_solution(836707984386906225)
XLA Ops:
  7.2 0.0 all-reduce.2.cloned.1.call-start
  7.2 10.0 %fusion.1 = f32[1024,1024]{1,0:T(8,128)} fusion(bf16[1024,2048]{1,0:T(8,128)(2,1)} %param.8, bf16[2048,1024]{1,0:T(8,128)(2,1)} %param.9), kind=kOutput, calls=%fused_computation.7 | convolution fusion | flops 4294967296 | bytes 12582912 | tf_op jit(solution)/shard_map/dot_general | solution.py:283
  17.2 15.2 %convolution_convert_fusion = bf16[1024,2048]{1,0:T(8,128)(2,1)} fusion(bf16[1024,2048]{1,0:T(8,128)(2,1)} %param.11, f32[1024,1024]{1,0:T(8,128)} %fusion.1, bf16[1024,2048]{1,0:T(8,128)(2,1)} %param.8, bf16[2048,1024]{1,0:T(8,128)(2,1)} %param.10), kind=kOutput, calls=%fused_computation.4 | convolution fusion | flops 8598323200 | bytes 20971520 | tf_op jit(solution)/shard_map/dot_general | solution.py:286
  32.3 0.0 all-reduce.2.cloned.1.call-update
  32.4 0.0 copy-start.6
  32.4 72.3 %all-reduce.2.cloned.1.call-done = bf16[1024,2048]{1,0:T(8,128)(2,1)} async-done(((bf16[1024,2048]{1,0:T(8,128)(2,1)}), bf16[1024,2048]{1,0:T(8,128)(2,1)}) %all-reduce.2.cloned.1.call-update) | async-done | bytes 4194320 | tf_op jit(solution)/shard_map/psum | solution.py:287
  104.6 0.0 copy-start.4
  104.6 0.0 copy-start.5
  104.6 5.0 %multiply_reduce_fusion = f32[1024]{0:T(1024)S(1)} fusion(bf16[1024,2048]{1,0:T(8,128)(2,1)} %all-reduce.2.cloned.1.call-done, bf16[1024,2048]{1,0:T(8,128)(2,1)} %param.8), kind=kLoop, calls=%fused_computation.1 | loop fusion | flops 10484736 | bytes 8392704 | tf_op jit(solution)/shard_map/reduce_sum | solution.py:289
  109.7 0.0 copy-done.6
  109.7 0.0 copy-done.4
  109.7 0.9 copy-done.5
  110.6 3.9 %multiply_convert_fusion.refs_0_ = bf16[1024,2048]{1,0:T(8,128)(2,1)} fusion(bf16[1024,2048]{1,0:T(8,128)(2,1)S(1)} %copy-done.5, bf16[1024,2048]{1,0:T(8,128)(2,1)S(1)} %copy-done.4, f32[1024]{0:T(1024)S(1)} %add_rsqrt_fusion, f32[2048]{0:T(1024)S(1)} %copy-done.6), kind=kLoop, calls=%fused_computation | loop fusion | flops 12582912 | bytes 12595200 | tf_op jit(solution)/shard_map/convert_element_type | solution.py:290
  114.5 52.9 %head0.1 = (f32[16288,512]{1,0:T(8,128)S(1)}, f32[8,512]{1,0:T(8,128)}) custom-call(bf16[1024,2048]{1,0:T(8,128)(2,1)} %multiply_convert_fusion.refs_0_, bf16[16032,2048]{1,0:T(8,128)(2,1)} %bitcast.13, f32[1,1024]{1,0:T(1,128)} %bitcast.15, s32[1,1024]{1,0:T(1,128)} %bitcast.17), custom_call_target="tpu_custom_call" | custom-call | flops 33621540864 | bytes 65667072 | tf_op jit(solution)/shard_map/head0/pallas_call | solution.py:257
  167.4 0.0 copy-start.3
  167.4 0.7 copy-done.3
  168.1 5.3 %exchange1.1.refs_4_.r0_ref = f32[8,512]{1,0:T(8,128)S(1)} custom-call(f32[8,512]{1,0:T(8,128)S(1)} %copy-done.3), custom_call_target="tpu_custom_call" | custom-call | tf_op jit(solution)/shard_map/exchange1/pallas_call | solution.py:264
  173.4 0.0 copy-start
  173.4 0.6 copy-done
  174.0 53.5 %head1.1 = (bf16[16032,1024]{1,0:T(8,128)(2,1)}, f32[16288,512]{1,0:T(8,128)S(1)}, f32[8,512]{1,0:T(8,128)}) custom-call(bf16[1024,2048]{1,0:T(8,128)(2,1)} %multiply_convert_fusion.refs_0_, bf16[16032,2048]{1,0:T(8,128)(2,1)} %bitcast.14, f32[1,1024]{1,0:T(1,128)} %bitcast.16, s32[1,1024]{1,0:T(1,128)} %bitcast.18, ...), custom_call_target="tpu_custom_call", output_to_operand_aliasing={{1}: (5, {})} | custom-call | flops 33621540864 | bytes 65667072 | tf_op jit(solution)/shard_map/head1/pallas_call | solution.py:257
  227.4 0.0 copy-start.2
  227.4 0.7 copy-done.2
  228.2 5.3 %exchange2.1.r1_ref = f32[8,512]{1,0:T(8,128)S(1)} custom-call(f32[8,512]{1,0:T(8,128)S(1)} %copy-done.2), custom_call_target="tpu_custom_call" | custom-call | tf_op jit(solution)/shard_map/exchange2/pallas_call | solution.py:264
  233.4 0.0 copy-start.1
  233.5 0.6 copy-done.1
  234.0 7.2 %finish.1 = (bf16[16032,1024]{1,0:T(8,128)(2,1)}, f32[1,1024]{1,0:T(1,128)}, f32[1,1024]{1,0:T(1,128)}, f32[1,1024]{1,0:T(1,128)}) custom-call(f32[16288,512]{1,0:T(8,128)S(1)} %get-tuple-element.15.l_ref, f32[8,512]{1,0:T(8,128)} %copy-done, f32[8,512]{1,0:T(8,128)} %copy-done.1, ...), custom_call_target="tpu_custom_call", output_to_operand_aliasing={{0}: (3, {})} | custom-call | tf_op jit(solution)/shard_map/finish/pallas_call | solution.py:272
  (1 shorter events, 0.0 us)
Async XLA Ops:
  7.2 97.5 %all-reduce.2.cloned.1.call-start = ((), (), s32[]{:S(2)}) async-start(), calls=%async_computation | async-start | bytes 8388608 | tf_op jit(solution)/shard_map/psum | solution.py:287
  32.4 77.3 %copy-start.6 = (f32[2048]{0:T(1024)S(1)}, f32[2048]{0:T(1024)}, u32[]{:S(2)}) copy-start(f32[2048]{0:T(1024)} %param.12) | copy-start | bytes 24580
  104.6 5.1 %copy-start.4 = (bf16[1024,2048]{1,0:T(8,128)(2,1)S(1)}, bf16[1024,2048]{1,0:T(8,128)(2,1)}, u32[]{:S(2)}) copy-start(bf16[1024,2048]{1,0:T(8,128)(2,1)} %param.8) | copy-start | bytes 12582916
  104.6 5.9 %copy-start.5 = (bf16[1024,2048]{1,0:T(8,128)(2,1)S(1)}, bf16[1024,2048]{1,0:T(8,128)(2,1)}, u32[]{:S(2)}) copy-start(bf16[1024,2048]{1,0:T(8,128)(2,1)} %all-reduce.2.cloned.1.call-done) | copy-start | bytes 12582916
  167.4 0.7 copy-start.3
  173.4 0.6 copy-start
  227.4 0.7 copy-start.2
  233.4 0.6 copy-start.1
Sparse Core Ops, SparseCore 0:
  32.5 72.1 all-reduce.1

commit v3 on v2

--- a/solution.py
+++ b/solution.py
@@ -18,7 +18,10 @@
 SB = 256
 SLICE = 128
 NB = 3
+CH = 256
+NQ = 4
 MIB = 2 ** 20
+FIRST_LIMIT = 31 * MIB
 LIMIT = 26 * MIB
 
 
@@ -94,73 +97,73 @@
         w_copy(wt_ref, wbuf, sems, tile, REM).start()
 
 
-def head_kernel(half, last_half, *refs):
-    if last_half:
-        (x_ref, wt_ref, t_ref, ids_ref, res_ref, l_in, o_ref, l_ref, stat_ref,
-         wbuf, st_ref, wsem, stage, osem) = refs
-    else:
-        x_ref, wt_ref, t_ref, ids_ref, l_ref, stat_ref, wbuf, st_ref, wsem = refs
-    for t in range(NB - 1):
-        w_copy(wt_ref, wbuf, wsem, t, BV).start()
-    init_stats(st_ref)
-    me = lax.axis_index('tp2') * 4 + lax.axis_index('tp')
-    inv_t = 1.0 / t_ref[:, half * R:(half + 1) * R]
-    ids = ids_ref[:, half * R:(half + 1) * R] - me * V
-    x = x_ref.at[pl.ds(half * R, R)]
+def head_loop(wt_ref, wbuf, wsem, x_ref, l_ref, st_ref, inv_t, ids, out=None, hooks=()):
+    if out is not None:
+        o_ref, col0, stage, osem, log_norm = out
 
     def out_copy(tile, size):
         slot = lax.rem(tile, 2) if not isinstance(tile, int) else tile % 2
         return pltpu.make_async_copy(stage.at[slot, pl.ds(0, size)],
-                                     o_ref.at[pl.ds(tile * BV, size), pl.ds((1 - half) * R, R)], osem.at[slot])
+                                     o_ref.at[pl.ds(tile * BV, size), pl.ds(col0, R)], osem.at[slot])
 
     def step(tile, size):
-        slot = lax.rem(tile, NB) if not isinstance(tile, int) else tile % NB
+        last = isinstance(tile, int)
+        slot = tile % NB if last else lax.rem(tile, NB)
         w_copy(wt_ref, wbuf, wsem, tile, size).wait()
-        if not isinstance(tile, int):
+        if not last:
             w_start(wt_ref, wbuf, wsem, tile + NB - 1)
         fin = None
-        if last_half:
-            oslot = lax.rem(tile, 2) if not isinstance(tile, int) else tile % 2
-            if isinstance(tile, int):
+        if out is not None:
+            if last:
                 out_copy(tile - 2, BV).wait()
             else:
                 @pl.when(tile >= 2)
                 def _():
                     out_copy(tile - 2, BV).wait()
-            fin = (stage.at[oslot], res_ref[0:1, :])
-        row0 = tile * BV if isinstance(tile, int) else pl.multiple_of(tile * BV, BV)
-        valid = None if isinstance(tile, int) else tile > 0
-        prev = head_tile(wbuf.at[slot], x, l_ref, st_ref, row0, size, inv_t, ids, fin, valid)
-        if isinstance(tile, int):
+            fin = (stage.at[tile % 2 if last else lax.rem(tile, 2)], log_norm)
+        row0 = tile * BV if last else pl.multiple_of(tile * BV, BV)
+        prev = head_tile(wbuf.at[slot], x_ref, l_ref, st_ref, row0, size, inv_t, ids, fin, None if last else tile > 0)
+        if last:
             block_stats(l_ref, st_ref, row0 + SB + size - prev, prev, ids)
-        if last_half:
+        if out is not None:
             out_copy(tile, size).start()
 
     def body(i, _):
+        for at, hook in hooks:
+            pl.when(i == at)(hook)
         step(i, BV)
         return 0
 
     lax.fori_loop(0, NT, body, 0)
     step(NT, REM)
-    reduce_stats(st_ref, stat_ref)
-    if last_half:
+    if out is not None:
         out_copy(NT - 1, BV).wait()
         out_copy(NT, REM).wait()
 
 
-def exchange_kernel(s_ref, res_ref, box, send_sem, recv_sem):
+def place():
     a, b = lax.axis_index('tp2'), lax.axis_index('tp')
+    return a, b // 2, b % 2
+
+
+PEERS = [(i, j) for i in range(2) for j in range(4) if (i, j) != (0, 0)]
+
+
+def peer(d):
+    a, b = lax.axis_index('tp2'), lax.axis_index('tp')
+    return {'tp2': (a + d[0]) % 2, 'tp': (b + d[1]) % 4}
+
+
+def barrier():
     bar = pltpu.get_barrier_semaphore()
-    peers = [(i, j) for i in range(2) for j in range(4) if (i, j) != (0, 0)]
-
-    def peer(d):
-        return {'tp2': lax.rem(a + d[0], 2), 'tp': lax.rem(b + d[1], 4)}
-
-    for d in peers:
+    for d in PEERS:
         pl.semaphore_signal(bar, inc=1, device_id=peer(d), device_id_type=MESH)
     pl.semaphore_wait(bar, 7)
+
+
+def exchange(s_ref, res_ref, box, send_sem, recv_sem):
     copies = []
-    for n, d in enumerate(peers):
+    for n, d in enumerate(PEERS):
         c = pltpu.make_async_remote_copy(s_ref, box.at[n], send_sem.at[n], recv_sem.at[n],
                                          device_id=peer(d), device_id_type=MESH)
         c.start()
@@ -184,6 +187,179 @@
     res_ref[3:8, :] = jnp.zeros((5, R), jnp.float32)
 
 
+def exchange_kernel(s_ref, res_ref, box, send_sem, recv_sem):
+    barrier()
+    exchange(s_ref, res_ref, box, send_sem, recv_sem)
+
+
+def first_kernel(h_ref, wg_ref, wu_ref, wd_ref, gain_ref, wt_ref, t_ref, ids_ref,
+                 l_ref, x1_ref, res_ref,
+                 wbuf, hbuf, hres, act, part, drecv, rbuf, x, st_ref, sbuf, box,
+                 wsem, msem, hsem, hrsem, dsem, rsem, gsem, fsem, xsem, esem):
+    y, xx, c = place()
+    g = 2 * y + xx
+    me = lax.axis_index('tp2') * 4 + lax.axis_index('tp')
+    half = CH // 2
+    own = half // 4
+
+    def weights(n):
+        src = (wg_ref, wu_ref)[n]
+        return [pltpu.make_async_copy(src.at[pl.ds(k * 1024, 1024)], wbuf.at[n, :, pl.ds(k * 1024, 1024)],
+                                      msem.at[2 * n + k]) for k in range(2)]
+
+    down = pltpu.make_async_copy(wd_ref, wbuf.at[2], msem.at[4])
+
+    def h_copy(q):
+        return pltpu.make_async_copy(h_ref.at[pl.ds(q * CH, CH)], hbuf, hsem)
+
+    def own_rows(q):
+        return pl.ds(q * CH + c * half + g * own, own)
+
+    def res_copy(q):
+        return pltpu.make_async_copy(h_ref.at[own_rows(q)], hres.at[q], hrsem.at[q])
+
+    def chip(d):
+        cx = (xx + d % 2) % 2
+        cy = (y + d // 2) % 2
+        return cy, cx, {'tp2': cy, 'tp': 2 * cx + c}
+
+    sibling = {'tp2': y, 'tp': 2 * xx + (c + 1) % 2}
+
+    def d_copy(q):
+        return pltpu.make_async_remote_copy(part.at[q, pl.ds(((c + 1) % 2) * half, half)], drecv.at[q],
+                                            dsem.at[0, q], dsem.at[1, q], device_id=sibling, device_id_type=MESH)
+
+    def r_copy(q, d):
+        cy, cx, dev = chip(d)
+        return pltpu.make_async_remote_copy(part.at[q, pl.ds(c * half + (2 * cy + cx) * own, own)], rbuf.at[q, d - 1],
+                                            rsem.at[0, q, d - 1], rsem.at[1, q, d - 1], device_id=dev,
+                                            device_id_type=MESH)
+
+    def g_copy(q, d):
+        return pltpu.make_async_remote_copy(x.at[own_rows(q)], x.at[own_rows(q)],
+                                            gsem.at[0, q, d - 1], gsem.at[1, q, d - 1], device_id=chip(d)[2],
+                                            device_id_type=MESH)
+
+    def f_copy(q):
+        rows = pl.ds(q * CH + c * half, half)
+        return pltpu.make_async_remote_copy(x.at[rows], x.at[rows], fsem.at[0, q], fsem.at[1, q],
+                                            device_id=sibling, device_id_type=MESH)
+
+    def pair_sum(q):
+        d_copy(q).wait()
+        rows = pl.ds(c * half, half)
+        part[q, rows, :] = (part[q, rows, :].astype(jnp.float32) + drecv[q].astype(jnp.float32)).astype(jnp.bfloat16)
+        for d in (3, 1, 2):
+            r_copy(q, d).start()
+
+    def total(q):
+        for d in (1, 2, 3):
+            r_copy(q, d).wait()
+        res_copy(q).wait()
+        mlp = part[q, pl.ds(c * half + g * own, own), :].astype(jnp.float32)
+        for d in range(3):
+            mlp += rbuf[q, d].astype(jnp.float32)
+        resid = hres[q].astype(jnp.float32) + mlp.astype(jnp.bfloat16).astype(jnp.float32)
+        inv_rms = lax.rsqrt(jnp.mean(resid * resid, axis=-1, keepdims=True) + NORM_EPS)
+        x[own_rows(q), :] = (gain_ref[...] * resid * inv_rms).astype(jnp.bfloat16)
+        for d in (3, 1, 2):
+            g_copy(q, d).start()
+
+    def gathered(q):
+        for d in (1, 2, 3):
+            g_copy(q, d).wait()
+        f_copy(q).start()
+
+    h_copy(0).start()
+    for n in range(2):
+        for cp in weights(n):
+            cp.start()
+    down.start()
+    for q in range(NQ):
+        res_copy(q).start()
+    init_stats(st_ref)
+    barrier()
+
+    def mlp(q, _):
+        h_copy(q).wait()
+
+        @pl.when(q == 0)
+        def _():
+            for n in range(2):
+                for cp in weights(n):
+                    cp.wait()
+        h = hbuf
+        for n in range(0, 1024, 512):
+            pre = [jnp.dot(h[:, 0:1024], wbuf[k, :, n:n + 512], preferred_element_type=jnp.float32)
+                   + jnp.dot(h[:, 1024:2048], wbuf[k, :, 1024 + n:1536 + n], preferred_element_type=jnp.float32)
+                   for k in range(2)]
+            act[:, n:n + 512] = (jax.nn.silu(pre[0]) * pre[1]).astype(jnp.bfloat16)
+
+        @pl.when(q + 1 < NQ)
+        def _():
+            h_copy(q + 1).start()
+
+        @pl.when(q == NQ - 1)
+        def _():
+            for t in range(NB - 1):
+                w_copy(wt_ref, wbuf, wsem, t, BV).start()
+
+        @pl.when(q == 0)
+        def _():
+            down.wait()
+        for n in range(0, 2048, 512):
+            part[q, :, n:n + 512] = jnp.dot(act[...], wbuf[2, :, n:n + 512],
+                                            preferred_element_type=jnp.float32).astype(jnp.bfloat16)
+        d_copy(q).start()
+
+        @pl.when((q >= 1) & (q <= NQ // 2))
+        def _():
+            pair_sum(q - 1)
+        return 0
+
+    lax.fori_loop(0, NQ, mlp, 0)
+    first = range(NQ // 2)
+    second = range(NQ // 2, NQ)
+    for q in first:
+        total(q)
+    for q in second:
+        pair_sum(q)
+    for q in first:
+        gathered(q)
+    for q in first:
+        f_copy(q).wait()
+
+    def x1_copy():
+        return pltpu.make_async_copy(x.at[pl.ds(R, R)], x1_ref, xsem)
+
+    def last_rows():
+        for q in second:
+            f_copy(q).wait()
+        x1_copy().start()
+
+    n2 = len(second)
+    hooks = [(2 + 2 * k, functools.partial(total, q)) for k, q in enumerate(second)]
+    hooks += [(3 + 2 * n2 + 2 * k, functools.partial(gathered, q)) for k, q in enumerate(second)]
+    hooks += [(4 + 4 * n2, last_rows)]
+    ids = ids_ref[:, 0:R] - me * V
+    head_loop(wt_ref, wbuf, wsem, x.at[pl.ds(0, R)], l_ref, st_ref, 1.0 / t_ref[:, 0:R], ids, hooks=hooks)
+    reduce_stats(st_ref, sbuf)
+    x1_copy().wait()
+    exchange(sbuf, res_ref, box, esem.at[0], esem.at[1])
+
+
+def second_kernel(x_ref, wt_ref, t_ref, ids_ref, res_ref, l_in, o_ref, l_ref, stat_ref,
+                  wbuf, st_ref, wsem, stage, osem):
+    for t in range(NB - 1):
+        w_copy(wt_ref, wbuf, wsem, t, BV).start()
+    init_stats(st_ref)
+    me = lax.axis_index('tp2') * 4 + lax.axis_index('tp')
+    ids = ids_ref[:, R:2 * R] - me * V
+    head_loop(wt_ref, wbuf, wsem, x_ref, l_ref, st_ref, 1.0 / t_ref[:, R:2 * R], ids,
+              out=(o_ref, 0, stage, osem, res_ref[0:1, :]))
+    reduce_stats(st_ref, stat_ref)
+
+
 def finish_kernel(l_ref, r0_ref, r1_ref, o_in, o_ref, ln_ref, en_ref, tl_ref, stage, osem):
     for half, r in ((0, r0_ref), (1, r1_ref)):
         cols = slice(half * R, (half + 1) * R)
@@ -236,28 +412,37 @@
     return pltpu.CompilerParams(has_side_effects=True, vmem_limit_bytes=limit, **kw)
 
 
-def head_call(half, x, wt, temp, ids, res=None, logits=None):
-    last = res is not None
-    l_type = VM((V + SB, R), jnp.float32)
-    stat_type = jax.ShapeDtypeStruct((8, R), jnp.float32)
-    scratch = [VM((NB, BV, 2048), jnp.bfloat16), VM((4, 8, R), jnp.float32), pltpu.SemaphoreType.DMA((NB,))]
-    if last:
-        args = (x, wt, temp, ids, res, in_vmem(logits))
-        in_specs = [vspec(), aspec(), vspec(), vspec(), vspec(), vspec()]
-        out_shape = (jax.ShapeDtypeStruct((V, 2 * R), jnp.bfloat16), l_type, stat_type)
-        out_specs = (aspec(), vspec(), vspec())
-        scratch += [VM((2, BV, R), jnp.bfloat16), pltpu.SemaphoreType.DMA((2,))]
-        alias = {5: 1}
-    else:
-        args = (x, wt, temp, ids)
-        in_specs = [vspec(), aspec(), vspec(), vspec()]
-        out_shape = (l_type, stat_type)
-        out_specs = (vspec(), vspec())
-        alias = {}
+L_TYPE = VM((V + SB, R), jnp.float32)
+HEAD_COST = pl.CostEstimate(flops=2 * V * R * 2048, bytes_accessed=V * 4096, transcendentals=V * R)
+
+
+def first_call(hidden, w_gate, w_up, w_down, gain, wt, temp, ids):
+    dma = pltpu.SemaphoreType.DMA
+    half, own = CH // 2, CH // 8
     return pl.pallas_call(
-        functools.partial(head_kernel, half, last), out_shape=out_shape, in_specs=in_specs, out_specs=out_specs,
-        scratch_shapes=scratch, input_output_aliases=alias, name='head%d' % half, compiler_params=params(LIMIT),
-        cost_estimate=pl.CostEstimate(flops=2 * V * R * 2048, bytes_accessed=V * 4096, transcendentals=V * R))(*args)
+        first_kernel,
+        out_shape=(L_TYPE, jax.ShapeDtypeStruct((R, 2048), jnp.bfloat16), jax.ShapeDtypeStruct((8, R), jnp.float32)),
+        in_specs=[aspec()] * 4 + [vspec(), aspec(), vspec(), vspec()], out_specs=(vspec(), aspec(), vspec()),
+        scratch_shapes=[
+            VM((NB, BV, 2048), jnp.bfloat16), VM((CH, 2048), jnp.bfloat16), VM((NQ, own, 2048), jnp.bfloat16),
+            VM((CH, 1024), jnp.bfloat16), VM((NQ, CH, 2048), jnp.bfloat16), VM((NQ, half, 2048), jnp.bfloat16),
+            VM((NQ, 3, own, 2048), jnp.bfloat16), VM((2 * R, 2048), jnp.bfloat16), VM((4, 8, R), jnp.float32),
+            VM((8, R), jnp.float32), VM((7, 8, R), jnp.float32),
+            dma((NB,)), dma((5,)), dma, dma((NQ,)), dma((2, NQ)), dma((2, NQ, 3)), dma((2, NQ, 3)), dma((2, NQ)),
+            dma, dma((2, 7))],
+        name='first', cost_estimate=HEAD_COST,
+        compiler_params=params(FIRST_LIMIT, collective_id=0))(hidden, w_gate, w_up, w_down, gain, wt, temp, ids)
+
+
+def second_call(x1, wt, temp, ids, res, logits):
+    return pl.pallas_call(
+        second_kernel,
+        out_shape=(jax.ShapeDtypeStruct((V, 2 * R), jnp.bfloat16), L_TYPE, jax.ShapeDtypeStruct((8, R), jnp.float32)),
+        in_specs=[vspec(), aspec(), vspec(), vspec(), vspec(), vspec()], out_specs=(aspec(), vspec(), vspec()),
+        scratch_shapes=[VM((NB, BV, 2048), jnp.bfloat16), VM((4, 8, R), jnp.float32), pltpu.SemaphoreType.DMA((NB,)),
+                        VM((2, BV, R), jnp.bfloat16), pltpu.SemaphoreType.DMA((2,))],
+        input_output_aliases={5: 1}, name='second', cost_estimate=HEAD_COST,
+        compiler_params=params(LIMIT))(x1, wt, temp, ids, res, in_vmem(logits))
 
 
 def exchange_call(stats, cid):
@@ -280,20 +465,11 @@
     model_axes = ('tp2', 'tp')
 
     def local_step(hidden, w_gate, w_up, w_down, norm_gain, w_vocab, temperature, target_ids):
-        gate_pre = jnp.dot(hidden, w_gate, preferred_element_type=jnp.float32)
-        up_pre = jnp.dot(hidden, w_up, preferred_element_type=jnp.float32)
-        hidden_act = (jax.nn.silu(gate_pre) * up_pre).astype(jnp.bfloat16)
-        part_out = jnp.dot(hidden_act, w_down, preferred_element_type=jnp.float32).astype(jnp.bfloat16)
-        mlp_out = lax.psum(part_out, model_axes)
-        resid_sum = hidden.astype(jnp.float32) + mlp_out.astype(jnp.float32)
-        inv_rms = lax.rsqrt(jnp.mean(resid_sum * resid_sum, axis=-1, keepdims=True) + NORM_EPS)
-        x = (norm_gain * resid_sum * inv_rms).astype(jnp.bfloat16)
         temp = temperature.reshape(1, 2 * R)
         ids = target_ids.reshape(1, 2 * R)
         wt = w_vocab.T
-        l0, s0 = head_call(0, x, wt, temp, ids)
-        r0 = exchange_call(s0, 1)
-        out, l1, s1 = head_call(1, x, wt, temp, ids, r0, l0)
+        l0, x1, r0 = first_call(hidden, w_gate, w_up, w_down, norm_gain.reshape(1, -1), wt, temp, ids)
+        out, l1, s1 = second_call(x1, wt, temp, ids, r0, l0)
         r1 = exchange_call(s1, 2)
         out, ln, en, tl = finish_call(l1, r0, r1, out)
         return ln.reshape(-1), en.reshape(-1), tl.reshape(-1), out.T

time: 248 us -> 164 us (0.66)
  waiting for transfers between devices: 72.3 us -> 0 us
  Pallas kernels: 124 us -> 162 us
  matrix products: 25.1 us -> 0 us
  between operations: 14.1 us -> 0.83 us
  other arithmetic: 8.96 us -> 0 us
    psum x1 -> x0, waiting for transfers between devices: 72.3 us -> none  [local_step(): mlp_out = lax.psum(part_out, model_axes)]
    pallas_call x2, Pallas kernels: 106 us -> 149 us  [the longest x1 95.6 us: first_call(): pl.pallas_call(first_kernel, out_shape=(L_TYPE, jax.ShapeDtypeStruct((R,...]
    dot_general x2 -> x0, matrix products: 25.1 us -> none  [the longest x1 15.2 us: local_step(): jnp.dot(hidden_act, w_down, preferred_element_type=jnp.float32)]
    reduce_sum x1 -> x0, other arithmetic: 5.02 us -> none  [local_step(): jnp.mean(resid_sum * resid_sum, axis=-1, keepdims=True) + NORM_EPS]
    pallas_call x2 -> x1, Pallas kernels: 10.6 us -> 5.84 us  [exchange_call(): pl.pallas_call(exchange_kernel, out_shape=jax.ShapeDtypeStruct((8, R), jn...]
    convert_element_type x1 -> x0, other arithmetic: 3.93 us -> none  [local_step(): x = (norm_gain * resid_sum * inv_rms).astype(jnp.bfloat16)]
  transfers between devices with their start and end apart: 1 -> 0, of which waited for: 1 -> 0; matrix products, arithmetic and copies ran while one was open for 0% -> 0% of each run, Pallas kernels for 0% -> 0%
where the time goes in v3:
time: 164 us
  Pallas kernels  162 us (99%)
    pallas_call x1, Pallas kernels, first_call(): pl.pallas_call(first_kernel, out_shape=(L_TYPE, jax.ShapeDtypeStruct((R,...  95.6 us
    pallas_call x1, Pallas kernels, second_call(): pl.pallas_call(second_kernel, out_shape=(jax.ShapeDtypeStruct((V, 2 * R),...  53.1 us
    pallas_call x1, Pallas kernels, finish_call(): pl.pallas_call(finish_kernel, out_shape=(jax.ShapeDtypeStruct((V, 2 * R),...  7.18 us
    pallas_call x1, Pallas kernels, exchange_call(): pl.pallas_call(exchange_kernel, out_shape=jax.ShapeDtypeStruct((8, R), jn...  5.84 us

profile of v3, /device:TPU:0, one launch (start us, length us, event | category | flops | bytes accessed | tf_op | source)
XLA Modules:
  0.0 163.8 jit_solution(13472518849053440678)
XLA Ops:
  0.6 95.6 %first.1 = (f32[16288,512]{1,0:T(8,128)S(1)}, bf16[512,2048]{1,0:T(8,128)(2,1)}, f32[8,512]{1,0:T(8,128)}) custom-call(bf16[1024,2048]{1,0:T(8,128)(2,1)} %h_ref.1, bf16[2048,1024]{1,0:T(8,128)(2,1)} %wg_ref.1, bf16[2048,1024]{1,0:T(8,128)(2,1)} %wu_ref.1, bf16[1024,2048]{1,0:T(8,128)(2,1)} %wd_ref.1, f32[1,2048]{1,0:T(1,128)} %bitcast.11, ...), custom_call_target="tpu_custom_call" | custom-call | flops 33621540864 | bytes 65667072 | tf_op jit(solution)/shard_map/first/pallas_call | solution.py:422
  96.3 53.1 %second.1 = (bf16[16032,1024]{1,0:T(8,128)(2,1)}, f32[16288,512]{1,0:T(8,128)S(1)}, f32[8,512]{1,0:T(8,128)}) custom-call(bf16[512,2048]{1,0:T(8,128)(2,1)} %get-tuple-element.14.x_ref, bf16[16032,2048]{1,0:T(8,128)(2,1)} %bitcast.10, f32[1,1024]{1,0:T(1,128)} %bitcast.13, s32[1,1024]{1,0:T(1,128)} %bitcast.15, ...), custom_call_target="tpu_custom_call", output_to_operand_aliasing={{1}: (5, {})} | custom-call | flops 33621540864 | bytes 65667072 | tf_op jit(solution)/shard_map/second/pallas_call | solution.py:438
  149.3 0.0 copy-start.1
  149.3 0.7 copy-done.1
  150.0 5.8 %exchange2.1.r1_ref = f32[8,512]{1,0:T(8,128)S(1)} custom-call(f32[8,512]{1,0:T(8,128)S(1)} %copy-done.1), custom_call_target="tpu_custom_call" | custom-call | tf_op jit(solution)/shard_map/exchange2/pallas_call | solution.py:449
  155.9 0.0 copy-start
  155.9 0.6 copy-done
  156.5 7.2 %finish.1 = (bf16[16032,1024]{1,0:T(8,128)(2,1)}, f32[1,1024]{1,0:T(1,128)}, f32[1,1024]{1,0:T(1,128)}, f32[1,1024]{1,0:T(1,128)}) custom-call(f32[16288,512]{1,0:T(8,128)S(1)} %get-tuple-element.17.l_ref, f32[8,512]{1,0:T(8,128)} %get-tuple-element.15.res_ref.r0_ref, f32[8,512]{1,0:T(8,128)} %copy-done, ...), custom_call_target="tpu_custom_call", output_to_operand_aliasing={{0}: (3, {})} | custom-call | tf_op jit(solution)/shard_map/finish/pallas_call | solution.py:457
Async XLA Ops:
  149.3 0.7 copy-start.1
  155.9 0.6 copy-start

commit v4 on v3

--- a/solution.py
+++ b/solution.py
@@ -15,33 +15,34 @@
 BV = 1024
 NT = V // BV
 REM = V - NT * BV
-SB = 256
+SB = 512
 SLICE = 128
 NB = 3
 CH = 256
 NQ = 4
 MIB = 2 ** 20
+LOG2E = 1.4426950408889634
 FIRST_LIMIT = 31 * MIB
 LIMIT = 26 * MIB
 
 
-def block_stats(l_ref, st_ref, row0, sb, ids, valid=None):
+def block_stats(l_ref, st_ref, row0, vocab0, sb, scale2, ids, valid=None):
     for c in range(0, R, 128):
         lanes = slice(c, c + 128)
+        a = scale2[:, lanes]
         m_old, s_old, q_old, t_old = (st_ref[n, :, lanes] for n in range(4))
         m, s, q, t = m_old, s_old, q_old, t_old
+        rel = ids[:, lanes] - vocab0 - lax.broadcasted_iota(jnp.int32, (8, 128), 0)
         for r in range(0, sb, SLICE):
             n = min(SLICE, sb - r) // 8
             l3 = l_ref[pl.ds(row0 + r, n * 8), lanes].reshape(n, 8, 128)
             m_new = jnp.maximum(m, jnp.max(l3, axis=0))
-            scale = jnp.exp(m - m_new)
-            e = jnp.exp(l3 - m_new[None])
-            shape = (n, 8, 128)
-            pos = lax.broadcasted_iota(jnp.int32, shape, 0) * 8 + lax.broadcasted_iota(jnp.int32, shape, 1)
-            hit = pos == (ids[:, lanes] - (row0 + r - SB))[None]
+            scale = jnp.exp2((m - m_new) * a)
+            e = jnp.exp2((l3 - m_new[None]) * a[None])
             s = s * scale + jnp.sum(e, axis=0)
             q = q * scale + jnp.sum(e * l3, axis=0)
-            t = t + jnp.sum(jnp.where(hit, l3, 0.0), axis=0)
+            for j in range(n):
+                t = jnp.where(rel == r + 8 * j, l3[j], t)
             m = m_new
         if valid is not None:
             m, s = jnp.where(valid, m, m_old), jnp.where(valid, s, s_old)
@@ -49,20 +50,18 @@
         st_ref[0, :, lanes], st_ref[1, :, lanes], st_ref[2, :, lanes], st_ref[3, :, lanes] = m, s, q, t
 
 
-def head_tile(w_ref, x_ref, l_ref, st_ref, row0, bv, inv_t, ids, fin=None, valid=None):
-    off, prev = 0, SB
-    while off < bv:
+def head_tile(w_ref, x_ref, l_ref, st_ref, row0, bv, prev0, scale2, ids, fin=None, valid=None):
+    for off in range(0, BV, SB):
+        block_stats(l_ref, st_ref, prev0 + off, prev0 + off, SB, scale2, ids, valid)
         sb = min(SB, bv - off)
-        rows = pl.ds(row0 + SB + off, sb)
+        if sb <= 0:
+            continue
+        rows = pl.ds(row0 + off, sb)
         if fin is not None:
-            stage, log_norm = fin
-            stage[pl.ds(off, sb), :] = (l_ref[rows, :] - log_norm).astype(jnp.bfloat16)
-        logits = lax.dot_general(w_ref[pl.ds(off, sb), :], x_ref[...], (((1,), (1,)), ((), ())),
-                                 preferred_element_type=jnp.float32) * inv_t
-        block_stats(l_ref, st_ref, row0 + SB + off - prev, prev, ids, valid if off == 0 else None)
-        l_ref[rows, :] = logits
-        off, prev = off + sb, sb
-    return prev
+            stage, inv_t, log_norm = fin
+            stage[pl.ds(off, sb), :] = (l_ref[rows, :] * inv_t - log_norm).astype(jnp.bfloat16)
+        l_ref[rows, :] = lax.dot_general(w_ref[pl.ds(off, sb), :], x_ref[...], (((1,), (1,)), ((), ())),
+                                         preferred_element_type=jnp.float32)
 
 
 def init_stats(st_ref):
@@ -72,13 +71,13 @@
     st_ref[3] = jnp.zeros((8, R), jnp.float32)
 
 
-def reduce_stats(st_ref, out_ref):
+def reduce_stats(st_ref, out_ref, inv_t):
     m = jnp.max(st_ref[0], axis=0, keepdims=True)
-    scale = jnp.exp(st_ref[0] - m)
-    out_ref[0:1, :] = m
+    scale = jnp.exp2((st_ref[0] - m) * (inv_t * LOG2E))
+    out_ref[0:1, :] = m * inv_t
     out_ref[1:2, :] = jnp.sum(st_ref[1] * scale, axis=0, keepdims=True)
-    out_ref[2:3, :] = jnp.sum(st_ref[2] * scale, axis=0, keepdims=True)
-    out_ref[3:4, :] = jnp.sum(st_ref[3], axis=0, keepdims=True)
+    out_ref[2:3, :] = jnp.sum(st_ref[2] * scale, axis=0, keepdims=True) * inv_t
+    out_ref[3:4, :] = jnp.sum(st_ref[3], axis=0, keepdims=True) * inv_t
     out_ref[4:8, :] = jnp.zeros((4, R), jnp.float32)
 
 
@@ -98,8 +97,9 @@
 
 
 def head_loop(wt_ref, wbuf, wsem, x_ref, l_ref, st_ref, inv_t, ids, out=None, hooks=()):
+    scale2 = inv_t * LOG2E
     if out is not None:
-        o_ref, col0, stage, osem, log_norm = out
+        o_ref, col0, stage, osem, out_inv_t, log_norm = out
 
     def out_copy(tile, size):
         slot = lax.rem(tile, 2) if not isinstance(tile, int) else tile % 2
@@ -120,11 +120,12 @@
                 @pl.when(tile >= 2)
                 def _():
                     out_copy(tile - 2, BV).wait()
-            fin = (stage.at[tile % 2 if last else lax.rem(tile, 2)], log_norm)
+            fin = (stage.at[tile % 2 if last else lax.rem(tile, 2)], out_inv_t, log_norm)
         row0 = tile * BV if last else pl.multiple_of(tile * BV, BV)
-        prev = head_tile(wbuf.at[slot], x_ref, l_ref, st_ref, row0, size, inv_t, ids, fin, None if last else tile > 0)
+        prev0 = row0 - BV if last else pl.multiple_of(jnp.maximum(row0 - BV, 0), BV)
+        head_tile(wbuf.at[slot], x_ref, l_ref, st_ref, row0, size, prev0, scale2, ids, fin, None if last else tile > 0)
         if last:
-            block_stats(l_ref, st_ref, row0 + SB + size - prev, prev, ids)
+            block_stats(l_ref, st_ref, row0, row0, size, scale2, ids)
         if out is not None:
             out_copy(tile, size).start()
 
@@ -343,7 +344,7 @@
     hooks += [(4 + 4 * n2, last_rows)]
     ids = ids_ref[:, 0:R] - me * V
     head_loop(wt_ref, wbuf, wsem, x.at[pl.ds(0, R)], l_ref, st_ref, 1.0 / t_ref[:, 0:R], ids, hooks=hooks)
-    reduce_stats(st_ref, sbuf)
+    reduce_stats(st_ref, sbuf, 1.0 / t_ref[:, 0:R])
     x1_copy().wait()
     exchange(sbuf, res_ref, box, esem.at[0], esem.at[1])
 
@@ -356,17 +357,18 @@
     me = lax.axis_index('tp2') * 4 + lax.axis_index('tp')
     ids = ids_ref[:, R:2 * R] - me * V
     head_loop(wt_ref, wbuf, wsem, x_ref, l_ref, st_ref, 1.0 / t_ref[:, R:2 * R], ids,
-              out=(o_ref, 0, stage, osem, res_ref[0:1, :]))
-    reduce_stats(st_ref, stat_ref)
-
-
-def finish_kernel(l_ref, r0_ref, r1_ref, o_in, o_ref, ln_ref, en_ref, tl_ref, stage, osem):
+              out=(o_ref, 0, stage, osem, 1.0 / t_ref[:, 0:R], res_ref[0:1, :]))
+    reduce_stats(st_ref, stat_ref, 1.0 / t_ref[:, R:2 * R])
+
+
+def finish_kernel(l_ref, r0_ref, r1_ref, t_ref, o_in, o_ref, ln_ref, en_ref, tl_ref, stage, osem):
     for half, r in ((0, r0_ref), (1, r1_ref)):
         cols = slice(half * R, (half + 1) * R)
         ln_ref[:, cols] = r[0:1, :]
         en_ref[:, cols] = r[1:2, :]
         tl_ref[:, cols] = r[2:3, :]
     log_norm = r1_ref[0:1, :]
+    inv_t = 1.0 / t_ref[:, R:2 * R]
 
     def out_copy(tile, size):
         slot = lax.rem(tile, 4) if not isinstance(tile, int) else tile % 4
@@ -382,7 +384,7 @@
             def _():
                 out_copy(tile - 4, BV).wait()
         row0 = tile * BV if isinstance(tile, int) else pl.multiple_of(tile * BV, BV)
-        stage[slot, 0:size, :] = (l_ref[pl.ds(row0 + SB, size), :] - log_norm).astype(jnp.bfloat16)
+        stage[slot, 0:size, :] = (l_ref[pl.ds(row0, size), :] * inv_t - log_norm).astype(jnp.bfloat16)
         out_copy(tile, size).start()
 
     def body(i, _):
@@ -412,7 +414,7 @@
     return pltpu.CompilerParams(has_side_effects=True, vmem_limit_bytes=limit, **kw)
 
 
-L_TYPE = VM((V + SB, R), jnp.float32)
+L_TYPE = VM((V, R), jnp.float32)
 HEAD_COST = pl.CostEstimate(flops=2 * V * R * 2048, bytes_accessed=V * 4096, transcendentals=V * R)
 
 
@@ -452,13 +454,13 @@
         name='exchange%d' % cid, compiler_params=params(LIMIT, collective_id=cid))(stats)
 
 
-def finish_call(logits, r0, r1, out):
+def finish_call(logits, r0, r1, temp, out):
     row = jax.ShapeDtypeStruct((1, 2 * R), jnp.float32)
     return pl.pallas_call(
         finish_kernel, out_shape=(jax.ShapeDtypeStruct((V, 2 * R), jnp.bfloat16), row, row, row),
-        in_specs=[vspec(), vspec(), vspec(), aspec()], out_specs=(aspec(), vspec(), vspec(), vspec()),
+        in_specs=[vspec(), vspec(), vspec(), vspec(), aspec()], out_specs=(aspec(), vspec(), vspec(), vspec()),
         scratch_shapes=[VM((4, BV, R), jnp.bfloat16), pltpu.SemaphoreType.DMA((4,))],
-        input_output_aliases={3: 0}, name='finish', compiler_params=params(LIMIT))(in_vmem(logits), r0, r1, out)
+        input_output_aliases={4: 0}, name='finish', compiler_params=params(LIMIT))(in_vmem(logits), r0, r1, temp, out)
 
 
 def solution(mesh):
@@ -471,7 +473,7 @@
         l0, x1, r0 = first_call(hidden, w_gate, w_up, w_down, norm_gain.reshape(1, -1), wt, temp, ids)
         out, l1, s1 = second_call(x1, wt, temp, ids, r0, l0)
         r1 = exchange_call(s1, 2)
-        out, ln, en, tl = finish_call(l1, r0, r1, out)
+        out, ln, en, tl = finish_call(l1, r0, r1, temp, out)
         return ln.reshape(-1), en.reshape(-1), tl.reshape(-1), out.T
 
     return jax.shard_map(

time: 164 us -> 157 us (0.957)
  Pallas kernels: 162 us -> 155 us
    pallas_call x1, Pallas kernels: 53.1 us -> 47.6 us  [second_call(): pl.pallas_call(second_kernel, out_shape=(jax.ShapeDtypeStruct((V, 2 * R),...]
where the time goes in v4:
time: 157 us
  Pallas kernels  155 us (99%)
    pallas_call x1, Pallas kernels, first_call(): pl.pallas_call(first_kernel, out_shape=(L_TYPE, jax.ShapeDtypeStruct((R,...  94.2 us
    pallas_call x1, Pallas kernels, second_call(): pl.pallas_call(second_kernel, out_shape=(jax.ShapeDtypeStruct((V, 2 * R),...  47.6 us
    pallas_call x1, Pallas kernels, finish_call(): pl.pallas_call(finish_kernel, out_shape=(jax.ShapeDtypeStruct((V, 2 * R),...  7.24 us
    pallas_call x1, Pallas kernels, exchange_call(): pl.pallas_call(exchange_kernel, out_shape=jax.ShapeDtypeStruct((8, R), jn...  5.83 us

profile of v4, /device:TPU:0, one launch (start us, length us, event | category | flops | bytes accessed | tf_op | source)
XLA Modules:
  0.0 157.1 jit_solution(3635868925679537240)
XLA Ops:
  0.6 94.2 %first.1 = (f32[16032,512]{1,0:T(8,128)S(1)}, bf16[512,2048]{1,0:T(8,128)(2,1)}, f32[8,512]{1,0:T(8,128)}) custom-call(bf16[1024,2048]{1,0:T(8,128)(2,1)} %h_ref.1, bf16[2048,1024]{1,0:T(8,128)(2,1)} %wg_ref.1, bf16[2048,1024]{1,0:T(8,128)(2,1)} %wu_ref.1, bf16[1024,2048]{1,0:T(8,128)(2,1)} %wd_ref.1, f32[1,2048]{1,0:T(1,128)} %bitcast.14, ...), custom_call_target="tpu_custom_call" | custom-call | flops 33621540864 | bytes 65667072 | tf_op jit(solution)/shard_map/first/pallas_call | solution.py:424
  94.9 47.6 %second.1 = (bf16[16032,1024]{1,0:T(8,128)(2,1)}, f32[16032,512]{1,0:T(8,128)S(1)}, f32[8,512]{1,0:T(8,128)}) custom-call(bf16[512,2048]{1,0:T(8,128)(2,1)} %get-tuple-element.14.x_ref, bf16[16032,2048]{1,0:T(8,128)(2,1)} %bitcast.13, f32[1,1024]{1,0:T(1,128)} %bitcast.10, s32[1,1024]{1,0:T(1,128)} %bitcast.16, ...), custom_call_target="tpu_custom_call", output_to_operand_aliasing={{1}: (5, {})} | custom-call | flops 33621540864 | bytes 65667072 | tf_op jit(solution)/shard_map/second/pallas_call | solution.py:440
  142.5 0.0 copy-start.1
  142.5 0.7 copy-done.1
  143.2 5.8 %exchange2.1.r1_ref = f32[8,512]{1,0:T(8,128)S(1)} custom-call(f32[8,512]{1,0:T(8,128)S(1)} %copy-done.1), custom_call_target="tpu_custom_call" | custom-call | tf_op jit(solution)/shard_map/exchange2/pallas_call | solution.py:451
  149.1 0.0 copy-start
  149.1 0.6 copy-done
  149.7 7.2 %finish.1 = (bf16[16032,1024]{1,0:T(8,128)(2,1)}, f32[1,1024]{1,0:T(1,128)}, f32[1,1024]{1,0:T(1,128)}, f32[1,1024]{1,0:T(1,128)}) custom-call(f32[16032,512]{1,0:T(8,128)S(1)} %get-tuple-element.17.l_ref, f32[8,512]{1,0:T(8,128)} %get-tuple-element.15.res_ref.r0_ref, f32[8,512]{1,0:T(8,128)} %copy-done, ...), custom_call_target="tpu_custom_call", output_to_operand_aliasing={{0}: (4, {})} | custom-call | tf_op jit(solution)/shard_map/finish/pallas_call | solution.py:459
Async XLA Ops:
  142.5 0.7 copy-start.1
  149.1 0.6 copy-start

commit v5 on v4

--- a/solution.py
+++ b/solution.py
@@ -18,16 +18,19 @@
 SB = 512
 SLICE = 128
 NB = 3
-CH = 256
-NQ = 4
+CH = 128
+NQ = 8
+LAG = 5
+EARLY = 7
+FV, FS = 512, 8
 MIB = 2 ** 20
 LOG2E = 1.4426950408889634
 FIRST_LIMIT = 31 * MIB
 LIMIT = 26 * MIB
 
 
-def block_stats(l_ref, st_ref, row0, vocab0, sb, scale2, ids, valid=None):
-    for c in range(0, R, 128):
+def block_stats(l_ref, st_ref, row0, vocab0, sb, scale2, ids, valid=None, span=(0, R)):
+    for c in range(span[0], span[1], 128):
         lanes = slice(c, c + 128)
         a = scale2[:, lanes]
         m_old, s_old, q_old, t_old = (st_ref[n, :, lanes] for n in range(4))
@@ -50,9 +53,9 @@
         st_ref[0, :, lanes], st_ref[1, :, lanes], st_ref[2, :, lanes], st_ref[3, :, lanes] = m, s, q, t
 
 
-def head_tile(w_ref, x_ref, l_ref, st_ref, row0, bv, prev0, scale2, ids, fin=None, valid=None):
+def head_tile(w_ref, x_ref, l_ref, st_ref, row0, bv, prev0, scale2, ids, fin=None, valid=None, span=(0, R)):
     for off in range(0, BV, SB):
-        block_stats(l_ref, st_ref, prev0 + off, prev0 + off, SB, scale2, ids, valid)
+        block_stats(l_ref, st_ref, prev0 + off, prev0 + off, SB, scale2, ids, valid, span)
         sb = min(SB, bv - off)
         if sb <= 0:
             continue
@@ -60,8 +63,8 @@
         if fin is not None:
             stage, inv_t, log_norm = fin
             stage[pl.ds(off, sb), :] = (l_ref[rows, :] * inv_t - log_norm).astype(jnp.bfloat16)
-        l_ref[rows, :] = lax.dot_general(w_ref[pl.ds(off, sb), :], x_ref[...], (((1,), (1,)), ((), ())),
-                                         preferred_element_type=jnp.float32)
+        l_ref[rows, span[0]:span[1]] = lax.dot_general(w_ref[pl.ds(off, sb), :], x_ref[span[0]:span[1], :], (((1,), (1,)), ((), ())),
+                                                       preferred_element_type=jnp.float32)
 
 
 def init_stats(st_ref):
@@ -81,22 +84,24 @@
     out_ref[4:8, :] = jnp.zeros((4, R), jnp.float32)
 
 
-def w_copy(wt_ref, wbuf, sems, tile, size):
-    slot = lax.rem(tile, NB) if not isinstance(tile, int) else tile % NB
+def w_copy(wt_ref, wbuf, sems, seq, size):
+    slot = seq % NB if isinstance(seq, int) else lax.rem(seq, NB)
+    tile = seq % (NT + 1) if isinstance(seq, int) else lax.rem(seq, NT + 1)
     return pltpu.make_async_copy(wt_ref.at[pl.ds(tile * BV, size)], wbuf.at[slot, pl.ds(0, size)], sems.at[slot])
 
 
-def w_start(wt_ref, wbuf, sems, tile):
-    @pl.when(tile < NT)
+def w_start(wt_ref, wbuf, sems, seq, end):
+    @pl.when((seq < end) & (seq != NT))
     def _():
-        w_copy(wt_ref, wbuf, sems, tile, BV).start()
-
-    @pl.when(tile == NT)
+        w_copy(wt_ref, wbuf, sems, seq, BV).start()
+
+    @pl.when(seq == NT)
     def _():
-        w_copy(wt_ref, wbuf, sems, tile, REM).start()
-
-
-def head_loop(wt_ref, wbuf, wsem, x_ref, l_ref, st_ref, inv_t, ids, out=None, hooks=()):
+        w_copy(wt_ref, wbuf, sems, seq, REM).start()
+
+
+def head_loop(wt_ref, wbuf, wsem, x_ref, l_ref, st_ref, inv_t, ids, out=None, hooks=(), first=0, count=NT + 1,
+              end=NT + 1, span=(0, R)):
     scale2 = inv_t * LOG2E
     if out is not None:
         o_ref, col0, stage, osem, out_inv_t, log_norm = out
@@ -106,12 +111,12 @@
         return pltpu.make_async_copy(stage.at[slot, pl.ds(0, size)],
                                      o_ref.at[pl.ds(tile * BV, size), pl.ds(col0, R)], osem.at[slot])
 
-    def step(tile, size):
-        last = isinstance(tile, int)
-        slot = tile % NB if last else lax.rem(tile, NB)
-        w_copy(wt_ref, wbuf, wsem, tile, size).wait()
-        if not last:
-            w_start(wt_ref, wbuf, wsem, tile + NB - 1)
+    def step(seq, size):
+        last = isinstance(seq, int)
+        slot = seq % NB if last else lax.rem(seq, NB)
+        tile = seq - (NT + 1 if first > NT else 0)
+        w_copy(wt_ref, wbuf, wsem, seq, size).wait()
+        w_start(wt_ref, wbuf, wsem, jnp.int32(seq + NB - 1), end)
         fin = None
         if out is not None:
             if last:
@@ -123,9 +128,8 @@
             fin = (stage.at[tile % 2 if last else lax.rem(tile, 2)], out_inv_t, log_norm)
         row0 = tile * BV if last else pl.multiple_of(tile * BV, BV)
         prev0 = row0 - BV if last else pl.multiple_of(jnp.maximum(row0 - BV, 0), BV)
-        head_tile(wbuf.at[slot], x_ref, l_ref, st_ref, row0, size, prev0, scale2, ids, fin, None if last else tile > 0)
-        if last:
-            block_stats(l_ref, st_ref, row0, row0, size, scale2, ids)
+        head_tile(wbuf.at[slot], x_ref, l_ref, st_ref, row0, size, prev0, scale2, ids, fin,
+                  None if last else seq > first, span)
         if out is not None:
             out_copy(tile, size).start()
 
@@ -135,8 +139,14 @@
         step(i, BV)
         return 0
 
-    lax.fori_loop(0, NT, body, 0)
-    step(NT, REM)
+    stop = min(first + count, NT) if first <= NT else first + count
+    lax.fori_loop(first, stop, body, 0)
+    if first <= NT < first + count:
+        step(NT, REM)
+        row0, size = NT * BV, REM
+    else:
+        row0, size = (stop - 1) % (NT + 1) * BV, BV
+    block_stats(l_ref, st_ref, row0, row0, size, scale2, ids, span=span)
     if out is not None:
         out_copy(NT - 1, BV).wait()
         out_copy(NT, REM).wait()
@@ -308,42 +318,52 @@
         @pl.when(q == 0)
         def _():
             down.wait()
+
+        @pl.when((q >= 1) & (q <= NQ // 2))
+        def _():
+            pair_sum(q - 1)
         for n in range(0, 2048, 512):
             part[q, :, n:n + 512] = jnp.dot(act[...], wbuf[2, :, n:n + 512],
                                             preferred_element_type=jnp.float32).astype(jnp.bfloat16)
         d_copy(q).start()
 
-        @pl.when((q >= 1) & (q <= NQ // 2))
+        @pl.when(q >= LAG)
         def _():
-            pair_sum(q - 1)
+            total(q - LAG)
         return 0
 
     lax.fori_loop(0, NQ, mlp, 0)
-    first = range(NQ // 2)
-    second = range(NQ // 2, NQ)
-    for q in first:
+    first, second, third = range(NQ // 4), range(NQ // 4, NQ // 2), range(NQ // 2, NQ)
+    for q in range(NQ - LAG, NQ // 2):
         total(q)
-    for q in second:
-        pair_sum(q)
     for q in first:
         gathered(q)
     for q in first:
         f_copy(q).wait()
+    ids = ids_ref[:, 0:R] - me * V
+    head = functools.partial(head_loop, wt_ref, wbuf, wsem, x.at[pl.ds(0, R)], l_ref, st_ref, 1.0 / t_ref[:, 0:R], ids,
+                             end=NT + 1 + EARLY)
+    head(first=0, count=EARLY, span=(0, R // 2))
+    for q in second:
+        gathered(q)
+    for q in third:
+        pair_sum(q)
+    for q in second:
+        f_copy(q).wait()
 
     def x1_copy():
         return pltpu.make_async_copy(x.at[pl.ds(R, R)], x1_ref, xsem)
 
     def last_rows():
-        for q in second:
+        for q in third:
             f_copy(q).wait()
         x1_copy().start()
 
-    n2 = len(second)
-    hooks = [(2 + 2 * k, functools.partial(total, q)) for k, q in enumerate(second)]
-    hooks += [(3 + 2 * n2 + 2 * k, functools.partial(gathered, q)) for k, q in enumerate(second)]
-    hooks += [(4 + 4 * n2, last_rows)]
-    ids = ids_ref[:, 0:R] - me * V
-    head_loop(wt_ref, wbuf, wsem, x.at[pl.ds(0, R)], l_ref, st_ref, 1.0 / t_ref[:, 0:R], ids, hooks=hooks)
+    hooks = [(EARLY + 1 + k, functools.partial(total, q)) for k, q in enumerate(third)]
+    head(first=EARLY, count=NT + 1 - EARLY, hooks=hooks)
+    for q in third:
+        gathered(q)
+    head(first=NT + 1, count=EARLY, span=(R // 2, R), hooks=[(NT + 1 + EARLY - 2, last_rows)])
     reduce_stats(st_ref, sbuf, 1.0 / t_ref[:, 0:R])
     x1_copy().wait()
     exchange(sbuf, res_ref, box, esem.at[0], esem.at[1])
@@ -371,31 +391,32 @@
     inv_t = 1.0 / t_ref[:, R:2 * R]
 
     def out_copy(tile, size):
-        slot = lax.rem(tile, 4) if not isinstance(tile, int) else tile % 4
+        slot = tile % FS if isinstance(tile, int) else lax.rem(tile, FS)
         return pltpu.make_async_copy(stage.at[slot, pl.ds(0, size)],
-                                     o_ref.at[pl.ds(tile * BV, size), pl.ds(R, R)], osem.at[slot])
+                                     o_ref.at[pl.ds(tile * FV, size), pl.ds(R, R)], osem.at[slot])
 
     def step(tile, size):
-        slot = lax.rem(tile, 4) if not isinstance(tile, int) else tile % 4
+        slot = tile % FS if isinstance(tile, int) else lax.rem(tile, FS)
         if isinstance(tile, int):
-            out_copy(tile - 4, BV).wait()
+            out_copy(tile - FS, FV).wait()
         else:
-            @pl.when(tile >= 4)
+            @pl.when(tile >= FS)
             def _():
-                out_copy(tile - 4, BV).wait()
-        row0 = tile * BV if isinstance(tile, int) else pl.multiple_of(tile * BV, BV)
+                out_copy(tile - FS, FV).wait()
+        row0 = tile * FV if isinstance(tile, int) else pl.multiple_of(tile * FV, FV)
         stage[slot, 0:size, :] = (l_ref[pl.ds(row0, size), :] * inv_t - log_norm).astype(jnp.bfloat16)
         out_copy(tile, size).start()
 
     def body(i, _):
-        step(i, BV)
+        step(i, FV)
         return 0
 
-    lax.fori_loop(0, NT, body, 0)
-    step(NT, REM)
-    for t in range(NT - 3, NT):
-        out_copy(t, BV).wait()
-    out_copy(NT, REM).wait()
+    n = V // FV
+    lax.fori_loop(0, n, body, 0)
+    step(n, V - n * FV)
+    for t in range(n + 1 - FS, n):
+        out_copy(t, FV).wait()
+    out_copy(n, V - n * FV).wait()
 
 
 def vspec():
@@ -459,7 +480,7 @@
     return pl.pallas_call(
         finish_kernel, out_shape=(jax.ShapeDtypeStruct((V, 2 * R), jnp.bfloat16), row, row, row),
         in_specs=[vspec(), vspec(), vspec(), vspec(), aspec()], out_specs=(aspec(), vspec(), vspec(), vspec()),
-        scratch_shapes=[VM((4, BV, R), jnp.bfloat16), pltpu.SemaphoreType.DMA((4,))],
+        scratch_shapes=[VM((FS, FV, R), jnp.bfloat16), pltpu.SemaphoreType.DMA((FS,))],
         input_output_aliases={4: 0}, name='finish', compiler_params=params(LIMIT))(in_vmem(logits), r0, r1, temp, out)
 
 

time: 157 us -> 152 us (0.968)
  Pallas kernels: 155 us -> 150 us
    pallas_call x1, Pallas kernels: 94.2 us -> 90.2 us  [first_call(): pl.pallas_call(first_kernel, out_shape=(L_TYPE, jax.ShapeDtypeStruct((R,...]
where the time goes in v5:
time: 152 us
  Pallas kernels  150 us (99%)
    pallas_call x1, Pallas kernels, first_call(): pl.pallas_call(first_kernel, out_shape=(L_TYPE, jax.ShapeDtypeStruct((R,...  90.2 us
    pallas_call x1, Pallas kernels, second_call(): pl.pallas_call(second_kernel, out_shape=(jax.ShapeDtypeStruct((V, 2 * R),...  47.4 us
    pallas_call x1, Pallas kernels, finish_call(): pl.pallas_call(finish_kernel, out_shape=(jax.ShapeDtypeStruct((V, 2 * R),...  7.16 us
    pallas_call x1, Pallas kernels, exchange_call(): pl.pallas_call(exchange_kernel, out_shape=jax.ShapeDtypeStruct((8, R), jn...  5.28 us

profile of v5, /device:TPU:0, one launch (start us, length us, event | category | flops | bytes accessed | tf_op | source)
XLA Modules:
  0.0 152.2 jit_solution(15137367340264983548)
XLA Ops:
  0.6 90.2 %first.1 = (f32[16032,512]{1,0:T(8,128)S(1)}, bf16[512,2048]{1,0:T(8,128)(2,1)}, f32[8,512]{1,0:T(8,128)}) custom-call(bf16[1024,2048]{1,0:T(8,128)(2,1)} %h_ref.1, bf16[2048,1024]{1,0:T(8,128)(2,1)} %wg_ref.1, bf16[2048,1024]{1,0:T(8,128)(2,1)} %wu_ref.1, bf16[1024,2048]{1,0:T(8,128)(2,1)} %wd_ref.1, f32[1,2048]{1,0:T(1,128)} %bitcast.14, ...), custom_call_target="tpu_custom_call" | custom-call | flops 33621540864 | bytes 65667072 | tf_op jit(solution)/shard_map/first/pallas_call | solution.py:445
  90.8 47.4 %second.1 = (bf16[16032,1024]{1,0:T(8,128)(2,1)}, f32[16032,512]{1,0:T(8,128)S(1)}, f32[8,512]{1,0:T(8,128)}) custom-call(bf16[512,2048]{1,0:T(8,128)(2,1)} %get-tuple-element.14.x_ref, bf16[16032,2048]{1,0:T(8,128)(2,1)} %bitcast.13, f32[1,1024]{1,0:T(1,128)} %bitcast.10, s32[1,1024]{1,0:T(1,128)} %bitcast.16, ...), custom_call_target="tpu_custom_call", output_to_operand_aliasing={{1}: (5, {})} | custom-call | flops 33621540864 | bytes 65667072 | tf_op jit(solution)/shard_map/second/pallas_call | solution.py:461
  138.3 0.0 copy-start.1
  138.3 0.7 copy-done.1
  139.0 5.3 %exchange2.1.r1_ref = f32[8,512]{1,0:T(8,128)S(1)} custom-call(f32[8,512]{1,0:T(8,128)S(1)} %copy-done.1), custom_call_target="tpu_custom_call" | custom-call | tf_op jit(solution)/shard_map/exchange2/pallas_call | solution.py:472
  144.3 0.0 copy-start
  144.3 0.6 copy-done
  144.9 7.2 %finish.1 = (bf16[16032,1024]{1,0:T(8,128)(2,1)}, f32[1,1024]{1,0:T(1,128)}, f32[1,1024]{1,0:T(1,128)}, f32[1,1024]{1,0:T(1,128)}) custom-call(f32[16032,512]{1,0:T(8,128)S(1)} %get-tuple-element.17.l_ref, f32[8,512]{1,0:T(8,128)} %get-tuple-element.15.res_ref.r0_ref, f32[8,512]{1,0:T(8,128)} %copy-done, ...), custom_call_target="tpu_custom_call", output_to_operand_aliasing={{0}: (4, {})} | custom-call | tf_op jit(solution)/shard_map/finish/pallas_call | solution.py:480
Async XLA Ops:
  138.3 0.7 copy-start.1
  144.3 0.6 copy-start

commit v6 on v5

--- a/solution.py
+++ b/solution.py
@@ -20,7 +20,7 @@
 NB = 3
 CH = 128
 NQ = 8
-LAG = 5
+LAG = 4
 EARLY = 7
 FV, FS = 512, 8
 MIB = 2 ** 20
@@ -54,17 +54,28 @@
 
 
 def head_tile(w_ref, x_ref, l_ref, st_ref, row0, bv, prev0, scale2, ids, fin=None, valid=None, span=(0, R)):
-    for off in range(0, BV, SB):
-        block_stats(l_ref, st_ref, prev0 + off, prev0 + off, SB, scale2, ids, valid, span)
-        sb = min(SB, bv - off)
+    def stats(off, n):
+        block_stats(l_ref, st_ref, prev0 + off, prev0 + off, n, scale2, ids, valid, span)
+
+    def dot(off, n):
+        sb = min(n, bv - off)
         if sb <= 0:
-            continue
+            return
         rows = pl.ds(row0 + off, sb)
         if fin is not None:
             stage, inv_t, log_norm = fin
             stage[pl.ds(off, sb), :] = (l_ref[rows, :] * inv_t - log_norm).astype(jnp.bfloat16)
-        l_ref[rows, span[0]:span[1]] = lax.dot_general(w_ref[pl.ds(off, sb), :], x_ref[span[0]:span[1], :], (((1,), (1,)), ((), ())),
-                                                       preferred_element_type=jnp.float32)
+        l_ref[rows, span[0]:span[1]] = lax.dot_general(w_ref[pl.ds(off, sb), :], x_ref[span[0]:span[1], :],
+                                                       (((1,), (1,)), ((), ())), preferred_element_type=jnp.float32)
+
+    if fin is not None:
+        dot(0, SB)
+        stats(0, BV)
+        dot(SB, SB)
+    else:
+        for off in range(0, BV, SB // 2):
+            stats(off, SB // 2)
+            dot(off, SB // 2)
 
 
 def init_stats(st_ref):
@@ -198,8 +209,11 @@
     res_ref[3:8, :] = jnp.zeros((5, R), jnp.float32)
 
 
-def exchange_kernel(s_ref, res_ref, box, send_sem, recv_sem):
+def exchange_kernel(s_any, res_ref, box, send_sem, recv_sem, s_ref, s_sem):
+    s_copy = pltpu.make_async_copy(s_any, s_ref, s_sem)
+    s_copy.start()
     barrier()
+    s_copy.wait()
     exchange(s_ref, res_ref, box, send_sem, recv_sem)
 
 
@@ -369,11 +383,15 @@
     exchange(sbuf, res_ref, box, esem.at[0], esem.at[1])
 
 
-def second_kernel(x_ref, wt_ref, t_ref, ids_ref, res_ref, l_in, o_ref, l_ref, stat_ref,
-                  wbuf, st_ref, wsem, stage, osem):
-    for t in range(NB - 1):
+def second_kernel(x_any, wt_ref, t_ref, ids_ref, res_ref, l_in, o_ref, l_ref, stat_ref,
+                  wbuf, st_ref, wsem, stage, osem, x_ref, xsem):
+    x_copy = pltpu.make_async_copy(x_any, x_ref, xsem)
+    w_copy(wt_ref, wbuf, wsem, 0, BV).start()
+    x_copy.start()
+    for t in range(1, NB - 1):
         w_copy(wt_ref, wbuf, wsem, t, BV).start()
     init_stats(st_ref)
+    x_copy.wait()
     me = lax.axis_index('tp2') * 4 + lax.axis_index('tp')
     ids = ids_ref[:, R:2 * R] - me * V
     head_loop(wt_ref, wbuf, wsem, x_ref, l_ref, st_ref, 1.0 / t_ref[:, R:2 * R], ids,
@@ -461,18 +479,21 @@
     return pl.pallas_call(
         second_kernel,
         out_shape=(jax.ShapeDtypeStruct((V, 2 * R), jnp.bfloat16), L_TYPE, jax.ShapeDtypeStruct((8, R), jnp.float32)),
-        in_specs=[vspec(), aspec(), vspec(), vspec(), vspec(), vspec()], out_specs=(aspec(), vspec(), vspec()),
+        in_specs=[aspec(), aspec(), vspec(), vspec(), vspec(), vspec()], out_specs=(aspec(), vspec(), vspec()),
         scratch_shapes=[VM((NB, BV, 2048), jnp.bfloat16), VM((4, 8, R), jnp.float32), pltpu.SemaphoreType.DMA((NB,)),
-                        VM((2, BV, R), jnp.bfloat16), pltpu.SemaphoreType.DMA((2,))],
+                        VM((2, BV, R), jnp.bfloat16), pltpu.SemaphoreType.DMA((2,)),
+                        VM((R, 2048), jnp.bfloat16), pltpu.SemaphoreType.DMA],
         input_output_aliases={5: 1}, name='second', cost_estimate=HEAD_COST,
         compiler_params=params(LIMIT))(x1, wt, temp, ids, res, in_vmem(logits))
 
 
 def exchange_call(stats, cid):
     return pl.pallas_call(
-        exchange_kernel, out_shape=jax.ShapeDtypeStruct((8, R), jnp.float32), in_specs=[vspec()], out_specs=vspec(),
-        scratch_shapes=[VM((7, 8, R), jnp.float32), pltpu.SemaphoreType.DMA((7,)), pltpu.SemaphoreType.DMA((7,))],
-        name='exchange%d' % cid, compiler_params=params(LIMIT, collective_id=cid))(stats)
+        exchange_kernel, out_shape=jax.ShapeDtypeStruct((8, R), jnp.float32), in_specs=[aspec()], out_specs=vspec(),
+        scratch_shapes=[VM((7, 8, R), jnp.float32), pltpu.SemaphoreType.DMA((7,)), pltpu.SemaphoreType.DMA((7,)),
+                        VM((8, R), jnp.float32), pltpu.SemaphoreType.DMA],
+        name='exchange%d' % cid, compiler_params=params(LIMIT, collective_id=cid))(
+            pltpu.with_memory_space_constraint(stats, pltpu.HBM))
 
 
 def finish_call(logits, r0, r1, temp, out):

time: 152 us -> 149 us (0.980)
  Pallas kernels: 150 us -> 147 us
    pallas_call x1, Pallas kernels: 90.2 us -> 88.5 us  [first_call(): pl.pallas_call(first_kernel, out_shape=(L_TYPE, jax.ShapeDtypeStruct((R,...]
where the time goes in v6:
time: 149 us
  Pallas kernels  147 us (99%)
    pallas_call x1, Pallas kernels, first_call(): pl.pallas_call(first_kernel, out_shape=(L_TYPE, jax.ShapeDtypeStruct((R,...  88.5 us
    pallas_call x1, Pallas kernels, second_call(): pl.pallas_call(second_kernel, out_shape=(jax.ShapeDtypeStruct((V, 2 * R),...  46.1 us
    pallas_call x1, Pallas kernels, finish_call(): pl.pallas_call(finish_kernel, out_shape=(jax.ShapeDtypeStruct((V, 2 * R),...  7.16 us
    pallas_call x1, Pallas kernels, exchange_call(): pl.pallas_call(exchange_kernel, out_shape=jax.ShapeDtypeStruct((8, R), jn...  5.34 us

profile of v6, /device:TPU:0, one launch (start us, length us, event | category | flops | bytes accessed | tf_op | source)
XLA Modules:
  0.0 148.5 jit_solution(7938918258038173706)
XLA Ops:
  0.6 88.5 %first.1 = (f32[16032,512]{1,0:T(8,128)S(1)}, bf16[512,2048]{1,0:T(8,128)(2,1)}, f32[8,512]{1,0:T(8,128)}) custom-call(bf16[1024,2048]{1,0:T(8,128)(2,1)} %h_ref.1, bf16[2048,1024]{1,0:T(8,128)(2,1)} %wg_ref.1, bf16[2048,1024]{1,0:T(8,128)(2,1)} %wu_ref.1, bf16[1024,2048]{1,0:T(8,128)(2,1)} %wd_ref.1, f32[1,2048]{1,0:T(1,128)} %bitcast.14, ...), custom_call_target="tpu_custom_call" | custom-call | flops 33621540864 | bytes 65667072 | tf_op jit(solution)/shard_map/first/pallas_call | solution.py:463
  89.2 46.1 %second.1 = (bf16[16032,1024]{1,0:T(8,128)(2,1)}, f32[16032,512]{1,0:T(8,128)S(1)}, f32[8,512]{1,0:T(8,128)}) custom-call(bf16[512,2048]{1,0:T(8,128)(2,1)} %get-tuple-element.14.x_any, bf16[16032,2048]{1,0:T(8,128)(2,1)} %bitcast.13, f32[1,1024]{1,0:T(1,128)} %bitcast.10, s32[1,1024]{1,0:T(1,128)} %bitcast.16, ...), custom_call_target="tpu_custom_call", output_to_operand_aliasing={{1}: (5, {})} | custom-call | flops 33621540864 | bytes 65667072 | tf_op jit(solution)/shard_map/second/pallas_call | solution.py:479
  135.3 5.3 %exchange2.1.r1_ref = f32[8,512]{1,0:T(8,128)S(1)} custom-call(f32[8,512]{1,0:T(8,128)} %get-tuple-element.18.s_any), custom_call_target="tpu_custom_call" | custom-call | tf_op jit(solution)/shard_map/exchange2/pallas_call | solution.py:491
  140.6 0.0 copy-start
  140.6 0.6 copy-done
  141.2 7.2 %finish.1 = (bf16[16032,1024]{1,0:T(8,128)(2,1)}, f32[1,1024]{1,0:T(1,128)}, f32[1,1024]{1,0:T(1,128)}, f32[1,1024]{1,0:T(1,128)}) custom-call(f32[16032,512]{1,0:T(8,128)S(1)} %get-tuple-element.17.l_ref, f32[8,512]{1,0:T(8,128)} %get-tuple-element.15.res_ref.r0_ref, f32[8,512]{1,0:T(8,128)} %copy-done, ...), custom_call_target="tpu_custom_call", output_to_operand_aliasing={{0}: (4, {})} | custom-call | tf_op jit(solution)/shard_map/finish/pallas_call | solution.py:501
Async XLA Ops:
  140.6 0.6 copy-start

commit v7 on v6

--- a/solution.py
+++ b/solution.py
@@ -21,7 +21,7 @@
 CH = 128
 NQ = 8
 LAG = 4
-EARLY = 7
+EARLY = 8
 FV, FS = 512, 8
 MIB = 2 ** 20
 LOG2E = 1.4426950408889634
@@ -373,7 +373,7 @@
             f_copy(q).wait()
         x1_copy().start()
 
-    hooks = [(EARLY + 1 + k, functools.partial(total, q)) for k, q in enumerate(third)]
+    hooks = [(EARLY + 2 + k, functools.partial(total, q)) for k, q in enumerate(third)]
     head(first=EARLY, count=NT + 1 - EARLY, hooks=hooks)
     for q in third:
         gathered(q)

time: 149 us -> 147 us (0.987)
    pallas_call x1, Pallas kernels: 88.5 us -> 86.8 us  [first_call(): pl.pallas_call(first_kernel, out_shape=(L_TYPE, jax.ShapeDtypeStruct((R,...]
where the time goes in v7:
time: 147 us
  Pallas kernels  146 us (99%)
    pallas_call x1, Pallas kernels, first_call(): pl.pallas_call(first_kernel, out_shape=(L_TYPE, jax.ShapeDtypeStruct((R,...  86.8 us
    pallas_call x1, Pallas kernels, second_call(): pl.pallas_call(second_kernel, out_shape=(jax.ShapeDtypeStruct((V, 2 * R),...  46.1 us
    pallas_call x1, Pallas kernels, finish_call(): pl.pallas_call(finish_kernel, out_shape=(jax.ShapeDtypeStruct((V, 2 * R),...  7.16 us
    pallas_call x1, Pallas kernels, exchange_call(): pl.pallas_call(exchange_kernel, out_shape=jax.ShapeDtypeStruct((8, R), jn...  5.59 us

profile of v7, /device:TPU:0, one launch (start us, length us, event | category | flops | bytes accessed | tf_op | source)
XLA Modules:
  0.0 147.1 jit_solution(4010446454338231878)
XLA Ops:
  0.6 86.8 %first.1 = (f32[16032,512]{1,0:T(8,128)S(1)}, bf16[512,2048]{1,0:T(8,128)(2,1)}, f32[8,512]{1,0:T(8,128)}) custom-call(bf16[1024,2048]{1,0:T(8,128)(2,1)} %h_ref.1, bf16[2048,1024]{1,0:T(8,128)(2,1)} %wg_ref.1, bf16[2048,1024]{1,0:T(8,128)(2,1)} %wu_ref.1, bf16[1024,2048]{1,0:T(8,128)(2,1)} %wd_ref.1, f32[1,2048]{1,0:T(1,128)} %bitcast.14, ...), custom_call_target="tpu_custom_call" | custom-call | flops 33621540864 | bytes 65667072 | tf_op jit(solution)/shard_map/first/pallas_call | solution.py:463
  87.4 46.1 %second.1 = (bf16[16032,1024]{1,0:T(8,128)(2,1)}, f32[16032,512]{1,0:T(8,128)S(1)}, f32[8,512]{1,0:T(8,128)}) custom-call(bf16[512,2048]{1,0:T(8,128)(2,1)} %get-tuple-element.14.x_any, bf16[16032,2048]{1,0:T(8,128)(2,1)} %bitcast.13, f32[1,1024]{1,0:T(1,128)} %bitcast.10, s32[1,1024]{1,0:T(1,128)} %bitcast.16, ...), custom_call_target="tpu_custom_call", output_to_operand_aliasing={{1}: (5, {})} | custom-call | flops 33621540864 | bytes 65667072 | tf_op jit(solution)/shard_map/second/pallas_call | solution.py:479
  133.5 5.6 %exchange2.1.r1_ref = f32[8,512]{1,0:T(8,128)S(1)} custom-call(f32[8,512]{1,0:T(8,128)} %get-tuple-element.18.s_any), custom_call_target="tpu_custom_call" | custom-call | tf_op jit(solution)/shard_map/exchange2/pallas_call | solution.py:491
  139.1 0.0 copy-start
  139.1 0.6 copy-done
  139.7 7.2 %finish.1 = (bf16[16032,1024]{1,0:T(8,128)(2,1)}, f32[1,1024]{1,0:T(1,128)}, f32[1,1024]{1,0:T(1,128)}, f32[1,1024]{1,0:T(1,128)}) custom-call(f32[16032,512]{1,0:T(8,128)S(1)} %get-tuple-element.17.l_ref, f32[8,512]{1,0:T(8,128)} %get-tuple-element.15.res_ref.r0_ref, f32[8,512]{1,0:T(8,128)} %copy-done, ...), custom_call_target="tpu_custom_call", output_to_operand_aliasing={{0}: (4, {})} | custom-call | tf_op jit(solution)/shard_map/finish/pallas_call | solution.py:501
Async XLA Ops:
  139.1 0.6 copy-start
